TPU v7x, 32 devices: a whole 2x2x4 slice. The times are simulated.
32 devices in a mesh: band: 16 (over z, y, core), spin: 2 (over x).
Axes of the slice: x: 2, y: 2, z: 4, core: 2. Of those that a mesh axis runs over, the one named last changes fastest.
Arguments:
- coefficients: bfloat16 [2, 2, 32, 524288], P('spin', None, 'band'), may hold values from -1 to 1
- occupation: int32 [2, 32], P('spin', 'band'), may hold values from 0 to 1000
- miller: int32 [3, 524288], P(None, ('band', 'spin')), may hold values from -8 to 8
- density: float32 [2, 256, 128, 128], P('spin', 'band'), may hold values from 0.25 to 2
- local_factor: float32 [2, 256, 128, 128], P(None, None, 'band'), may hold values from -1.2 to 1.2
Outputs:
- stress: float32 [6], replicated
- kinetic_density: float32 [524288], P(('band', 'spin'))
- gradient_square: float32 [2, 256, 128, 128], P('spin', 'band')
All inputs are finite; a program needn't handle non-finite values.
Results may differ from a plain program's by a relative error of at most 0.0003.
Values sent between devices are 32-bit elements; how exact they have to be, the bound alone decides.
A program may use at most 64 MiB of HBM per device.

v0:
```python
import jax
import jax.numpy as jnp
from jax import lax
from jax.sharding import PartitionSpec as P

NPW = 524288
NX = 128
NY = 128
NZ = 256


occupation_unit = 1000.0
kpoint = (0.25, 0.125, 0.375)
spacing = 0.25


def derivative_table(length):
    row_index = jnp.arange(length, dtype=jnp.int32)[:, None]
    col_index = jnp.arange(length, dtype=jnp.int32)[None, :]
    wrapped = jnp.mod(row_index - col_index, length)
    angles = jnp.pi / length * wrapped.astype(jnp.float32)
    on_diagonal = wrapped == 0
    sines = jnp.where(on_diagonal, 1.0, jnp.sin(angles))
    parity = 1.0 - 2.0 * jnp.mod(wrapped, 2).astype(jnp.float32)
    return jnp.where(on_diagonal, 0.0, 0.5 * parity * jnp.cos(angles) / sines)


def fourier_tables(length):
    positions = jnp.arange(length, dtype=jnp.int32)
    phases = jnp.mod(positions[:, None] * positions[None, :], length).astype(jnp.float32) * (
        2.0 * jnp.pi / length
    )
    return (jnp.cos(phases), jnp.sin(phases))


def frequencies(length):
    positions = jnp.arange(length, dtype=jnp.int32)
    signed = jnp.where(positions >= length // 2, positions - length, positions)
    return 2.0 * jnp.pi / length * signed.astype(jnp.float32)


def six_sums(weighting, first_axis, second_axis, third_axis):
    return jnp.stack(
        [
            jnp.sum(weighting * first_axis * first_axis),
            jnp.sum(weighting * second_axis * second_axis),
            jnp.sum(weighting * third_axis * third_axis),
            jnp.sum(weighting * second_axis * third_axis),
            jnp.sum(weighting * first_axis * third_axis),
            jnp.sum(weighting * first_axis * second_axis),
        ]
    )


def xc_terms(dens_part, grad_x, grad_y, grad_z, cell_count):
    square = grad_x * grad_x + grad_y * grad_y + grad_z * grad_z
    kernel = dens_part ** (-1.0 / 3.0) / (1.0 + square / (4.0 * dens_part * dens_part + 1.0))
    return (square, -six_sums(kernel, grad_x, grad_y, grad_z) / cell_count)


def shards(coefficients, occupation, miller, density, local_factor):
    highest = lax.Precision.HIGHEST
    weights = occupation.astype(jnp.float32) / occupation_unit
    piece = coefficients.astype(jnp.float32)
    squares = piece[0, 0] * piece[0, 0] + piece[0, 1] * piece[0, 1]
    kinetic_weight = lax.psum_scatter(
        jnp.dot(weights[0], squares, precision=highest),
        ("band", "spin"),
        scatter_dimension=0,
        tiled=True,
    )
    kvec = jnp.array(kpoint, jnp.float32)
    gvec = spacing * (miller.astype(jnp.float32) + kvec[:, None])
    kinetic_density = 0.5 * (gvec[0] ** 2 + gvec[1] ** 2 + gvec[2] ** 2) * kinetic_weight
    kinetic_stress = -six_sums(kinetic_weight, gvec[0], gvec[1], gvec[2]) / NPW
    band_devices = lax.axis_size("band")
    cell_count = density.shape[1] * band_devices * density.shape[2] * density.shape[3]
    deriv_x = derivative_table(NX)
    deriv_y = derivative_table(NY)
    deriv_z = derivative_table(NZ)
    cosine_x, sine_x = fourier_tables(NX)
    cosine_y, sine_y = fourier_tables(NY)
    cosine_z, sine_z = fourier_tables(NZ)
    grad_x = jnp.einsum("ik,szky->sziy", deriv_x, density, precision=highest)
    grad_y = jnp.einsum("ik,szxk->szxi", deriv_y, density, precision=highest)
    along_real = jnp.einsum("mj,szxj->szxm", cosine_y, density, precision=highest)
    along_imag = -jnp.einsum("mj,szxj->szxm", sine_y, density, precision=highest)
    plane_real = jnp.einsum("mj,szjy->szmy", cosine_x, along_real, precision=highest) + jnp.einsum(
        "mj,szjy->szmy", sine_x, along_imag, precision=highest
    )
    plane_imag = jnp.einsum("mj,szjy->szmy", cosine_x, along_imag, precision=highest) - jnp.einsum(
        "mj,szjy->szmy", sine_x, along_real, precision=highest
    )
    dens_col, real_col, imag_col = (
        lax.all_to_all(density, "band", split_axis=2, concat_axis=1, tiled=True),
        lax.all_to_all(plane_real, "band", split_axis=2, concat_axis=1, tiled=True),
        lax.all_to_all(plane_imag, "band", split_axis=2, concat_axis=1, tiled=True),
    )
    gradz_col = jnp.einsum("ik,skxy->sixy", deriv_z, dens_col, precision=highest)
    grad_z = lax.all_to_all(gradz_col, "band", split_axis=1, concat_axis=2, tiled=True)
    gradient_square, xc_stress = xc_terms(density, grad_x, grad_y, grad_z, cell_count)
    spec_real = (
        jnp.einsum("mj,jxy->mxy", cosine_z, real_col[0], precision=highest)
        + jnp.einsum("mj,jxy->mxy", sine_z, imag_col[0], precision=highest)
    ) / cell_count
    spec_imag = (
        jnp.einsum("mj,jxy->mxy", cosine_z, imag_col[0], precision=highest)
        - jnp.einsum("mj,jxy->mxy", sine_z, real_col[0], precision=highest)
    ) / cell_count
    total_real, total_imag = lax.psum((spec_real, spec_imag), "spin")
    local_rows = real_col.shape[2]
    first_column = lax.axis_index("band") * local_rows
    freq_z = frequencies(NZ)[:, None, None]
    freq_x = lax.dynamic_slice_in_dim(frequencies(NX), first_column, local_rows, 0)[None, :, None]
    freq_y = frequencies(NY)[None, None, :]
    length_sq = freq_x * freq_x + freq_y * freq_y + freq_z * freq_z
    positive = length_sq > 0
    inverse = jnp.where(positive, 1.0 / jnp.where(positive, length_sq, 1.0), 0.0)
    hartree_weight = 4.0 * jnp.pi * (total_real * total_real + total_imag * total_imag) * inverse
    diagonal = jnp.array([1.0, 1.0, 1.0, 0.0, 0.0, 0.0], jnp.float32)
    hartree_stress = 2.0 * six_sums(
        hartree_weight * inverse, freq_x, freq_y, freq_z
    ) - diagonal * jnp.sum(hartree_weight)
    local_weight = 2.0 * (total_real * local_factor[0] + total_imag * local_factor[1])
    local_stress = six_sums(local_weight, freq_x, freq_y, freq_z)
    spin_share = 1.0 / lax.axis_size("spin")
    partial_stress = kinetic_stress + spin_share * (hartree_stress + local_stress) + xc_stress
    stress = lax.psum(partial_stress, ("band", "spin"))
    return (stress, kinetic_density, gradient_square)


def solution(mesh):
    return jax.shard_map(
        shards,
        mesh=mesh,
        in_specs=(
            P("spin", None, "band", None),
            P("spin", "band"),
            P(None, ("band", "spin")),
            P("spin", "band", None, None),
            P(None, None, "band", None),
        ),
        out_specs=(P(), P(("band", "spin")), P("spin", "band", None, None)),
        check_vma=False,
    )
```

profile of v0, /device:TPU:0, one launch (start us, length us, event | category | flops | bytes accessed | tf_op | source)
XLA Modules:
  0.0 327.8 jit_solution(17758232457839028548)
XLA Ops:
  7.2 2.5 fusion.6
  9.7 2.5 convolution_bitcast_fusion.2
  12.2 1.2 fusion.99
  13.4 1.2 fusion.4
  14.6 1.4 copy.29
  16.0 7.5 %all-to-all-start.1 = ((f32[1,16,128,128]{3,1,0,2:T(8,128)}), f32[1,16,128,128]{3,1,0,2:T(8,128)}, u32[]{:S(2)}, u32[]{:S(2)}) async-start(f32[1,16,128,128]{3,1,0,2:T(8,128)} %copy.29), calls=%async_computation.1 | async-start | bytes 2097152 | tf_op jit(solution)/shard_map/all_to_all | solution.py:97
  23.5 0.2 all-reduce.5.cloned.1.call-start
  23.8 4.7 %convert_element_type.102 = f32[1,2,2,524288]{3,2,1,0:T(2,128)S(1)} convert(bf16[1,2,2,524288]{3,2,1,0:T(2,128)(2,1)} %param.7) | non-fusion elementwise | flops 2097152 | bytes 12582912 | tf_op jit(solution)/shard_map/convert_element_type | solution.py:64
  28.5 17.0 %fusion.2 = f32[1,524288]{1,0:T(1,128)} fusion(f32[1,2,2,524288]{3,2,1,0:T(2,128)S(1)} %convert_element_type.102, s32[1,2]{1,0:T(1,128)S(1)} %copy-done.5), kind=kOutput, calls=%fused_computation.4 | convolution fusion | flops 15728644 | bytes 10485768 | tf_op jit(solution)/shard_map/dot_general | solution.py:67
  45.6 1.6 copy.35
  47.2 1.2 fusion.101
  48.4 1.2 fusion.5
  49.7 1.4 copy.26
  51.1 0.1 fusion.201
  51.2 6.0 %all-to-all-start = ((f32[1,16,128,128]{3,1,0,2:T(8,128)}), f32[1,16,128,128]{3,1,0,2:T(8,128)S(1)}, u32[]{:S(2)}, u32[]{:S(2)}) async-start(f32[1,16,128,128]{3,1,0,2:T(8,128)} %copy.26), calls=%async_computation | async-start | bytes 2097152 | tf_op jit(solution)/shard_map/all_to_all | solution.py:96
  57.2 0.1 add_multiply_fusion
  57.3 29.4 %all-to-all-done = f32[1,16,128,128]{3,1,0,2:T(8,128)S(1)} async-done(((f32[1,16,128,128]{3,1,0,2:T(8,128)}), f32[1,16,128,128]{3,1,0,2:T(8,128)S(1)}, u32[]{:S(2)}, u32[]{:S(2)}) %all-to-all-start) | async-done | bytes 1048608 | tf_op jit(solution)/shard_map/all_to_all | solution.py:96
  86.6 8.0 %all-to-all-start.2 = ((f32[1,16,128,128]{3,1,0,2:T(8,128)}), f32[1,16,128,128]{3,1,0,2:T(8,128)}, u32[]{:S(2)}, u32[]{:S(2)}) async-start(f32[1,16,128,128]{3,1,0,2:T(8,128)} %copy.35), calls=%async_computation.2 | async-start | bytes 2097152 | tf_op jit(solution)/shard_map/all_to_all | solution.py:95
  94.6 0.1 fusion.204
  94.7 1.6 copy.59
  96.4 0.6 copy.31
  97.0 0.3 copy.60
  97.3 0.6 copy.28
  98.0 21.6 %all-to-all-done.2 = f32[1,16,128,128]{3,1,0,2:T(8,128)} async-done(((f32[1,16,128,128]{3,1,0,2:T(8,128)}), f32[1,16,128,128]{3,1,0,2:T(8,128)}, u32[]{:S(2)}, u32[]{:S(2)}) %all-to-all-start.2) | async-done | bytes 1048608 | tf_op jit(solution)/shard_map/all_to_all | solution.py:95
  119.6 1.3 copy.36
  120.9 2.2 convolution_bitcast_fusion
  123.2 1.6 copy.37
  124.7 7.6 %all-to-all-start.3 = ((f32[1,256,8,128]{3,2,0,1:T(8,128)}), f32[1,256,8,128]{3,2,0,1:T(8,128)}, u32[]{:S(2)}, u32[]{:S(2)}) async-start(f32[1,256,8,128]{3,2,0,1:T(8,128)} %copy.37), calls=%async_computation.3 | async-start | bytes 2097152 | tf_op jit(solution)/shard_map/all_to_all | solution.py:100
  132.4 2.0 fusion.45
  134.4 2.0 fusion.47
  136.4 3.1 fusion.7
  139.5 3.0 fusion.8
  142.6 2.3 convolution_bitcast_fusion.1
  144.9 0.1 broadcast_add_fusion
  145.0 1.7 fusion.203
  146.7 57.4 %all-reduce.5.cloned.1.call-done = f32[524288]{0:T(1024)} async-done(((f32[524288]{0:T(1024)}), f32[524288]{0:T(1024)}) %all-reduce.5.cloned.1.call-update) | async-done | bytes 2097168
  204.0 2.2 multiply_reduce_fusion.13
  206.2 3.7 %stack.90 = f32[6]{0:T(128)S(1)} concatenate(f32[1]{0:T(128)} %bitcast.5, f32[1]{0:T(128)} %bitcast.7, f32[1]{0:T(128)} %bitcast.9, f32[1]{0:T(128)} %bitcast.10, f32[1]{0:T(128)} %bitcast.11, f32[1]{0:T(128)} %bitcast.12), dimensions={0} | concatenate | bytes 48 | tf_op jit(solution)/shard_map/stack | solution.py:43
  210.0 5.9 %fusion.14 = (f32[1,16,128,128]{3,2,1,0:T(8,128)S(1)}, f32[1,16,128,128]{3,2,1,0:T(8,128)}, f32[128,16,128]{0,2,1:T(8,128)S(1)}) fusion(f32[1,16,128,128]{3,2,1,0:T(8,128)S(1)} %copy-done, f32[1,16,16,8,128]{4,3,2,1,0:T(8,128)} %bitcast.57, f32[1,16,128,128]{3,2,1,0:T(8,128)} %convolution_bitcast_fusion.1), kind=kOutput, calls=%fused_computation.27 | convolution fusion | flops 406093824 | bytes 6291456 | tf_op jit(solution)/shard_map/ik,szxk->szxi/dot_general | solution.py:85
  215.9 2.4 fusion.20
  218.3 3.8 %stack.111 = f32[6]{0:T(128)S(1)} concatenate(f32[1]{0:T(128)} %bitcast.60, f32[1]{0:T(128)} %bitcast.62, f32[1]{0:T(128)} %bitcast.64, f32[1]{0:T(128)} %bitcast.65, f32[1]{0:T(128)} %bitcast.66, f32[1]{0:T(128)} %bitcast.68), dimensions={0} | concatenate | bytes 48 | tf_op jit(solution)/shard_map/stack | solution.py:43
  222.2 46.0 %all-reduce.7.cloned.1.call-done = (f32[256,8,128]{2,0,1:T(8,128)}, f32[256,8,128]{2,0,1:T(8,128)}) async-done(((f32[256,8,128]{2,0,1:T(8,128)}, f32[256,8,128]{2,0,1:T(8,128)}), (f32[256,8,128]{2,0,1:T(8,128)}, f32[256,8,128]{2,0,1:T(8,128)})) %all-reduce.7.cloned.1.call-update) | async-done | bytes 2097168 | tf_op jit(solution)/shard_map/psum | solution.py:110
  268.2 2.8 fusion.121
  271.0 1.9 multiply_reduce_fusion.2
  272.9 3.8 %stack.97 = f32[6]{0:T(128)S(1)} concatenate(f32[1]{0:T(128)} %bitcast.30, f32[1]{0:T(128)} %bitcast.31, f32[1]{0:T(128)} %bitcast.32, f32[1]{0:T(128)} %bitcast.33, f32[1]{0:T(128)} %bitcast.34, f32[1]{0:T(128)} %bitcast.35), dimensions={0} | concatenate | bytes 48 | tf_op jit(solution)/shard_map/stack | solution.py:43
  276.7 3.8 %stack.104 = f32[6]{0:T(128)S(1)} concatenate(f32[1]{0:T(128)} %bitcast.38, f32[1]{0:T(128)} %bitcast.39, f32[1]{0:T(128)} %bitcast.40, f32[1]{0:T(128)} %bitcast.41, f32[1]{0:T(128)} %bitcast.42, f32[1]{0:T(128)} %bitcast.43), dimensions={0} | concatenate | bytes 48 | tf_op jit(solution)/shard_map/stack | solution.py:43
  280.5 0.7 multiply_add_fusion
  281.2 39.3 %psum.23 = f32[6]{0:T(128)} all-reduce(f32[6]{0:T(128)S(1)} %multiply_add_fusion), channel_id=1, replica_groups=mesh['band'=16,'spin'=2] {'band','spin'}, use_global_device_ids=true, to_apply=%region_28.29 | all-reduce | flops 6 | bytes 48 | tf_op jit(solution)/shard_map/psum | solution.py:128
  (22 shorter events, 0.1 us)
Async XLA Ops:
  16.0 35.1 %all-to-all-start.1 = ((f32[1,16,128,128]{3,1,0,2:T(8,128)}), f32[1,16,128,128]{3,1,0,2:T(8,128)}, u32[]{:S(2)}, u32[]{:S(2)}) async-start(f32[1,16,128,128]{3,1,0,2:T(8,128)} %copy.29), calls=%async_computation.1 | async-start | bytes 2097152 | tf_op jit(solution)/shard_map/all_to_all | solution.py:97
  23.5 5.0 %copy-start.5 = (s32[1,2]{1,0:T(1,128)S(1)}, s32[1,2]{1,0:T(1,128)}, u32[]{:S(2)}) copy-start(s32[1,2]{1,0:T(1,128)} %param.8) | copy-start | bytes 28
  23.5 180.5 %all-reduce.5.cloned.1.call-start = ((), (), s32[]{:S(2)}) async-start(), calls=%async_computation.4 | async-start | bytes 4194304
  28.5 17.1 %copy-start = (f32[1,16,128,128]{3,2,1,0:T(8,128)S(1)}, f32[1,16,128,128]{3,2,1,0:T(8,128)}, u32[]{:S(2)}) copy-start(f32[1,16,128,128]{3,2,1,0:T(8,128)} %param.10) | copy-start | bytes 3145732
  48.4 8.7 %copy-start.2 = (s32[3,16384]{1,0:T(4,128)S(1)}, s32[3,16384]{1,0:T(4,128)}, u32[]{:S(2)}) copy-start(s32[3,16384]{1,0:T(4,128)} %param.9) | copy-start | bytes 589828
  48.4 8.7 %copy-start.3 = (f32[3]{0:T(128)S(1)}, f32[3]{0:T(128)}, u32[]{:S(2)}) copy-start(f32[3]{0:T(128)} %constant.139.clone) | copy-start | bytes 40
  51.2 35.5 %all-to-all-start = ((f32[1,16,128,128]{3,1,0,2:T(8,128)}), f32[1,16,128,128]{3,1,0,2:T(8,128)S(1)}, u32[]{:S(2)}, u32[]{:S(2)}) async-start(f32[1,16,128,128]{3,1,0,2:T(8,128)} %copy.26), calls=%async_computation | async-start | bytes 2097152 | tf_op jit(solution)/shard_map/all_to_all | solution.py:96
  86.6 32.9 %all-to-all-start.2 = ((f32[1,16,128,128]{3,1,0,2:T(8,128)}), f32[1,16,128,128]{3,1,0,2:T(8,128)}, u32[]{:S(2)}, u32[]{:S(2)}) async-start(f32[1,16,128,128]{3,1,0,2:T(8,128)} %copy.35), calls=%async_computation.2 | async-start | bytes 2097152 | tf_op jit(solution)/shard_map/all_to_all | solution.py:95
  124.7 85.2 %all-to-all-start.3 = ((f32[1,256,8,128]{3,2,0,1:T(8,128)}), f32[1,256,8,128]{3,2,0,1:T(8,128)}, u32[]{:S(2)}, u32[]{:S(2)}) async-start(f32[1,256,8,128]{3,2,0,1:T(8,128)} %copy.37), calls=%async_computation.3 | async-start | bytes 2097152 | tf_op jit(solution)/shard_map/all_to_all | solution.py:100
  132.3 135.8 %all-reduce.7.cloned.1.call-start = ((), (), s32[]{:S(2)}) async-start(), calls=%async_computation.5 | async-start | bytes 4194304 | tf_op jit(solution)/shard_map/psum | solution.py:110
  210.0 5.9 %copy-start.1 = (f32[1,16,128,128]{3,2,1,0:T(8,128)S(1)}, f32[1,16,128,128]{3,2,1,0:T(8,128)}, u32[]{:S(2)}) copy-start(f32[1,16,128,128]{3,2,1,0:T(8,128)} %convolution_bitcast_fusion.1) | copy-start | bytes 3145732
  268.1 12.4 %copy-start.4 = (f32[6]{0:T(128)S(1)}, f32[6]{0:T(128)}, u32[]{:S(2)}) copy-start(f32[6]{0:T(128)} %constant.140.clone) | copy-start | bytes 76
Sparse Core Ops, SparseCore 0:
  45.7 158.2 all-reduce.4
  206.4 61.7 all-reduce.6
where the time goes:
time: 333 us; the launch traced here: 328 us
  waiting for transfers between devices  154 us (46%)
  matrix products  47.6 us (14%)
  blocking collectives  39.3 us (12%)
  starting transfers between devices  29.2 us (9%)
  local copies, waits for them, and re-layouts  27.6 us (8%)
  other arithmetic  15.1 us (5%)
  between operations  14.7 us (4%)
    unnamed x3, waiting for transfers between devices  57.4 us
    psum x1, waiting for transfers between devices, shards(): total_real, total_imag = lax.psum((spec_real, spec_imag), 'spin')  46 us
    psum x1, blocking collectives, shards(): stress = lax.psum(partial_stress, ('band', 'spin'))  39.3 us
    all_to_all x1, waiting for transfers between devices, shards(): lax.all_to_all(plane_real, 'band', split_axis=2, concat_axis=1, tiled=True)  29.4 us
    all_to_all x1, waiting for transfers between devices, shards(): lax.all_to_all(density, 'band', split_axis=2, concat_axis=1, tiled=True)  21.6 us
    dot_general x1, matrix products, shards(): jnp.dot(weights[0], squares, precision=highest)  17 us
    another operation x4, local copies, waits for them, and re-layouts, six_sums(): jnp.stack([jnp.sum(weighting * first_axis * first_axis), jnp.sum(weightin...  15.2 us
    all_to_all x1, starting transfers between devices, shards(): lax.all_to_all(density, 'band', split_axis=2, concat_axis=1, tiled=True)  7.95 us
  transfers between devices with their start and end apart: 6, of which 4 were waited for; matrix products, arithmetic and copies ran while one was open for 21% of the time, Pallas kernels for 0%

commit v1 on v0

v1 whole, which is shorter than its diff:
```python
import functools

import jax
import jax.numpy as jnp
import numpy as np
from jax import lax
from jax.experimental import pallas as pl
from jax.experimental.pallas import tpu as pltpu
from jax.sharding import PartitionSpec as P

occupation_unit = 1000.0
kpoint = (0.25, 0.125, 0.375)
spacing = 0.25
MESH = pl.DeviceIdType.MESH
VMEM = pl.BlockSpec(memory_space=pltpu.VMEM)


def derivative_table(length):
    index = np.arange(length)
    wrapped = np.mod(index[:, None] - index[None, :], length)
    angles = np.pi / length * wrapped
    sines = np.where(wrapped == 0, 1.0, np.sin(angles))
    parity = 1.0 - 2.0 * np.mod(wrapped, 2)
    table = np.where(wrapped == 0, 0.0, 0.5 * parity * np.cos(angles) / sines)
    return table.astype(np.float32)


def fourier_tables(length):
    index = np.arange(length)
    phases = np.mod(index[:, None] * index[None, :], length) * (2.0 * np.pi / length)
    return np.cos(phases), np.sin(phases)


def frequencies(length):
    index = np.arange(length)
    signed = np.where(index >= length // 2, index - length, index)
    return (2.0 * np.pi / length * signed).astype(np.float32)


def six_rows(weighting, first_axis, second_axis, third_axis):
    dims = tuple(range(weighting.ndim - 1))
    wx, wy, wz = weighting * first_axis, weighting * second_axis, weighting * third_axis
    terms = (
        wx * first_axis,
        wy * second_axis,
        wz * third_axis,
        wy * third_axis,
        wx * third_axis,
        wx * second_axis,
    )
    return jnp.stack([jnp.sum(t, axis=dims) for t in terms])


def greet_all(nb, ns):
    b, s = lax.axis_index("band"), lax.axis_index("spin")
    barrier = pltpu.get_barrier_semaphore()

    def greet(k, carry):
        pl.semaphore_signal(
            barrier,
            inc=1,
            device_id=((b + k // ns) % nb, (s + k % ns) % ns),
            device_id_type=MESH,
        )
        return carry

    lax.fori_loop(1, nb * ns, greet, 0)
    pl.semaphore_wait(barrier, nb * ns - 1)
    return b, s


def far_first(k, count):
    return 1 + (k + count // 2 - 1) % (count - 1)


def first_kernel(
    nb, ns, ny, nz, dens, kin, dcol, half, kout,
    from_core, sum_core, from_plane, sum_plane, from_line,
    d_send, d_recv, h_send, h_recv, c_send, c_recv, p_send, p_recv, l_send, l_recv,
):
    b, s = greet_all(nb, ns)
    core, y, z = b % 2, (b // 2) % ny, b // (2 * ny)
    zh = dens.shape[0] // ns

    core_copy = pltpu.make_async_remote_copy(
        kin.at[:, :, 1 - core], from_core, c_send.at[0], c_recv.at[0],
        device_id=(b + 1 - 2 * core, s), device_id_type=MESH,
    )
    core_copy.start()

    half_copies = []
    for k in range(1, ns):
        other = (s + k) % ns
        half_copies.append(
            pltpu.make_async_remote_copy(
                dens.at[pl.ds(other * zh, zh)], half.at[k - 1], h_send.at[k - 1], h_recv.at[k - 1],
                device_id=(b, other), device_id_type=MESH,
            )
        )

    def column_copy(k):
        offset = far_first(k, nb)
        to = (b + offset) % nb
        return pltpu.make_async_remote_copy(
            dens.at[:, to], dcol.at[b], d_send.at[k], d_recv.at[k],
            device_id=(to, s), device_id_type=MESH,
        )

    def start_column(k, carry):
        column_copy(k).start()
        return carry

    lax.fori_loop(0, nb - 1, start_column, 0)
    for copy in half_copies:
        copy.start()
    dcol[b] = dens[:, b]

    core_copy.wait()
    sum_core[...] = kin[:, :, core] + from_core[...]
    plane_copies = []
    for k in range(1, ny * ns):
        ty, ts = (y + k // ns) % ny, (s + k % ns) % ns
        copy = pltpu.make_async_remote_copy(
            sum_core.at[:, ty, ts], from_plane.at[k - 1], p_send.at[k - 1], p_recv.at[k - 1],
            device_id=((z * ny + ty) * 2 + core, ts), device_id_type=MESH,
        )
        copy.start()
        plane_copies.append(copy)
    for copy in plane_copies:
        copy.wait()
    total = sum_core[:, y, s]
    for k in range(1, ny * ns):
        total = total + from_plane[k - 1]
    sum_plane[...] = total

    def line_copy(k):
        tz = (z + k) % nz
        return pltpu.make_async_remote_copy(
            sum_plane.at[tz], from_line.at[k - 1], l_send.at[k - 1], l_recv.at[k - 1],
            device_id=((tz * ny + y) * 2 + core, s), device_id_type=MESH,
        )

    def start_line(k, carry):
        line_copy(k).start()
        return carry

    def wait_line(k, carry):
        line_copy(k).wait()
        return carry

    lax.fori_loop(1, nz, start_line, 0)
    lax.fori_loop(1, nz, wait_line, 0)
    kout[...] = sum_plane[z] + jnp.sum(from_line[...], axis=0)

    for copy in half_copies:
        copy.wait()

    def wait_column(k, carry):
        column_copy(k).wait()
        return carry

    lax.fori_loop(0, nb - 1, wait_column, 0)


def second_kernel(nb, ns, spec, grad, scol, gout, s_send, s_recv, g_send, g_recv):
    b, s = greet_all(nb, ns)
    n = nb * ns

    def spec_copy(k):
        offset = far_first(k, n)
        tb, ts = (b + offset // ns) % nb, (s + offset % ns) % ns
        return pltpu.make_async_remote_copy(
            spec.at[ts, :, tb], scol.at[b, s], s_send.at[k], s_recv.at[k],
            device_id=(tb, ts), device_id_type=MESH,
        )

    def grad_copy(k):
        to = (b + far_first(k, nb)) % nb
        return pltpu.make_async_remote_copy(
            grad.at[to], gout.at[:, b], g_send.at[k], g_recv.at[k],
            device_id=(to, s), device_id_type=MESH,
        )

    def start_grad(k, carry):
        grad_copy(k).start()
        return carry

    def start_spec(k, carry):
        spec_copy(k).start()
        return carry

    lax.fori_loop(0, nb - 1, start_grad, 0)
    lax.fori_loop(0, n - 1, start_spec, 0)
    gout[:, b] = grad[b]
    scol[b, s] = spec[s, :, b]

    def wait_grad(k, carry):
        grad_copy(k).wait()
        return carry

    def wait_spec(k, carry):
        spec_copy(k).wait()
        return carry

    lax.fori_loop(0, nb - 1, wait_grad, 0)
    lax.fori_loop(0, n - 1, wait_spec, 0)


def third_kernel(nb, ns, part, out, held, send, recv):
    b, s = greet_all(nb, ns)
    n = nb * ns

    def copy_of(k):
        tb, ts = (b + k // ns) % nb, (s + k % ns) % ns
        return pltpu.make_async_remote_copy(
            part, held.at[k - 1], send.at[k - 1], recv.at[k - 1],
            device_id=(tb, ts), device_id_type=MESH,
        )

    def start(k, carry):
        copy_of(k).start()
        return carry

    def wait(k, carry):
        copy_of(k).wait()
        return carry

    lax.fori_loop(1, n, start, 0)
    lax.fori_loop(1, n, wait, 0)
    out[...] = part[...] + jnp.sum(held[...], axis=0)


def params(number):
    return pltpu.CompilerParams(
        collective_id=number, has_side_effects=True, vmem_limit_bytes=40 * 2**20
    )


def f32(*shape):
    return jax.ShapeDtypeStruct(shape, jnp.float32)


def shards(nb, ns, coefficients, occupation, miller, density, local_factor):
    high = lax.Precision.HIGH
    dma = pltpu.SemaphoreType.DMA
    _, zl, nx, ny = density.shape
    nzg = zl * nb
    xl = nx // nb
    zh = zl // ns
    lanes = 2 * ny // ns
    cells = nzg * nx * ny
    npw = coefficients.shape[3]
    rows = npw // (nb * ns * 128)
    fold_y = 2 if nb % 4 == 0 else 1
    fold_z = nb // (2 * fold_y)
    b, s = lax.axis_index("band"), lax.axis_index("spin")

    weights = occupation[0].astype(jnp.float32) / occupation_unit
    piece = coefficients[0].astype(jnp.float32)
    kin = jnp.sum(weights[:, None] * (piece[0] * piece[0] + piece[1] * piece[1]), axis=0)
    kin = kin.reshape(fold_z, fold_y, 2, ns, rows, 128)
    dens = density[0]

    dcol, half, kinetic_weight = pl.pallas_call(
        functools.partial(first_kernel, nb, ns, fold_y, fold_z),
        out_shape=(f32(nb, zl, xl, ny), f32(ns - 1, zh, nb, xl, ny), f32(rows, 128)),
        in_specs=[VMEM] * 2,
        out_specs=(VMEM,) * 3,
        scratch_shapes=[
            pltpu.VMEM((fold_z, fold_y, ns, rows, 128), jnp.float32),
            pltpu.VMEM((fold_z, fold_y, ns, rows, 128), jnp.float32),
            pltpu.VMEM((fold_y * ns - 1, fold_z, rows, 128), jnp.float32),
            pltpu.VMEM((fold_z, rows, 128), jnp.float32),
            pltpu.VMEM((fold_z - 1, rows, 128), jnp.float32),
            dma((nb - 1,)), dma((nb - 1,)), dma((ns - 1,)), dma((ns - 1,)), dma((1,)), dma((1,)),
            dma((fold_y * ns - 1,)), dma((fold_y * ns - 1,)), dma((fold_z - 1,)), dma((fold_z - 1,)),
        ],
        compiler_params=params(0),
        name="first_exchange",
    )(dens.reshape(zl, nb, xl, ny), kin)

    own = lax.dynamic_slice_in_dim(dens, s * zh, zh, 0)
    total = own + jnp.sum(half, axis=0).reshape(zh, nx, ny)
    cos_x, sin_x = fourier_tables(nx)
    cos_y, sin_y = fourier_tables(ny)
    cos_z, sin_z = fourier_tables(nzg)
    along = jnp.concatenate(
        [
            jnp.einsum("mj,zjy->zmy", cos_x.astype(np.float32), total, precision=high),
            jnp.einsum("mj,zjy->zmy", (-sin_x).astype(np.float32), total, precision=high),
        ],
        axis=2,
    ).reshape(zh * nx, 2 * ny)
    part = ny // ns
    planes = []
    for k in range(ns):
        cut = slice(k * part, (k + 1) * part)
        table = np.block([[cos_y[:, cut], -sin_y[:, cut]], [sin_y[:, cut], cos_y[:, cut]]])
        planes.append(jnp.dot(along, table.astype(np.float32), precision=high))
    spec = jnp.stack(planes).reshape(ns, zh, nb, xl, lanes)

    grad_col = jnp.dot(derivative_table(nzg), dcol.reshape(nzg, xl * ny), precision=high)

    scol, gout = pl.pallas_call(
        functools.partial(second_kernel, nb, ns),
        out_shape=(f32(nb, ns, zh, xl, lanes), f32(zl, nb, xl, ny)),
        in_specs=[VMEM] * 2,
        out_specs=(VMEM,) * 2,
        scratch_shapes=[
            dma((nb * ns - 1,)), dma((nb * ns - 1,)), dma((nb - 1,)), dma((nb - 1,)),
        ],
        compiler_params=params(1),
        name="second_exchange",
    )(spec, grad_col.reshape(nb, zl, xl, ny))

    gvec = spacing * (miller.astype(jnp.float32) + jnp.array(kpoint, jnp.float32)[:, None])
    gvec = gvec.reshape(3, rows, 128)
    kinetic_density = (
        0.5 * (gvec[0] ** 2 + gvec[1] ** 2 + gvec[2] ** 2) * kinetic_weight
    ).reshape(rows * 128)
    stress_rows = -six_rows(kinetic_weight, gvec[0], gvec[1], gvec[2]) / npw

    grad_x = jnp.einsum("ik,zky->ziy", derivative_table(nx), dens, precision=high)
    grad_y = jnp.einsum("ik,zxk->zxi", derivative_table(ny), dens, precision=high)
    grad_z = gout.reshape(zl, nx, ny)
    square = grad_x * grad_x + grad_y * grad_y + grad_z * grad_z
    kernel = dens ** (-1.0 / 3.0) / (1.0 + square / (4.0 * dens * dens + 1.0))
    stress_rows = stress_rows - six_rows(kernel, grad_x, grad_y, grad_z) / cells

    tables = (np.concatenate([cos_z, sin_z]) / cells).astype(np.float32)
    turned = jnp.dot(tables, scol.reshape(nzg, xl * lanes), precision=high)
    turned = turned.reshape(2, nzg, xl, lanes)
    real = turned[0, :, :, :part] + turned[1, :, :, part:]
    imag = turned[0, :, :, part:] - turned[1, :, :, :part]
    spectrum = jnp.concatenate([real, imag], axis=2)
    factor = lax.dynamic_slice_in_dim(local_factor, s * part, part, 3)
    factor = jnp.concatenate([factor[0], factor[1]], axis=2)
    freq_z = frequencies(nzg)[:, None, None]
    freq_x = lax.dynamic_slice_in_dim(jnp.asarray(frequencies(nx)), b * xl, xl, 0)[None, :, None]
    freq_y = lax.dynamic_slice_in_dim(jnp.asarray(frequencies(ny)), s * part, part, 0)
    freq_y = jnp.concatenate([freq_y, freq_y])[None, None, :]
    length_sq = freq_x * freq_x + freq_y * freq_y + freq_z * freq_z
    positive = length_sq > 0
    inverse = jnp.where(positive, 1.0 / jnp.where(positive, length_sq, 1.0), 0.0)
    hartree = 4.0 * jnp.pi * spectrum * spectrum * inverse
    weight = 2.0 * (hartree * inverse + spectrum * factor)
    spec_rows = six_rows(weight, freq_x, freq_y, freq_z)
    diagonal = np.array([1.0, 1.0, 1.0, 0.0, 0.0, 0.0], np.float32)[:, None]
    spec_rows = spec_rows - diagonal * jnp.sum(hartree, axis=(0, 1))[None]
    stress_rows = stress_rows + spec_rows

    stress = pl.pallas_call(
        functools.partial(third_kernel, nb, ns),
        out_shape=f32(8, 128),
        in_specs=[VMEM],
        out_specs=VMEM,
        scratch_shapes=[
            pltpu.VMEM((nb * ns - 1, 8, 128), jnp.float32),
            dma((nb * ns - 1,)), dma((nb * ns - 1,)),
        ],
        compiler_params=params(2),
        name="stress_sum",
    )(jnp.concatenate([stress_rows, jnp.zeros((2, 128), jnp.float32)]))
    return (jnp.sum(stress[:6], axis=1), kinetic_density, square[None])


def solution(mesh):
    return jax.shard_map(
        functools.partial(shards, mesh.shape["band"], mesh.shape["spin"]),
        mesh=mesh,
        in_specs=(
            P("spin", None, "band", None),
            P("spin", "band"),
            P(None, ("band", "spin")),
            P("spin", "band", None, None),
            P(None, None, "band", None),
        ),
        out_specs=(P(), P(("band", "spin")), P("spin", "band", None, None)),
        check_vma=False,
    )
```

time: 333 us -> 153 us (0.46); the launches traced: 328 us -> 153 us
  waiting for transfers between devices: 154 us -> 0 us
  Pallas kernels: 0 us -> 102 us
  blocking collectives: 39.3 us -> 0 us
  matrix products: 47.6 us -> 8.48 us
  starting transfers between devices: 29.2 us -> 0 us
  local copies, waits for them, and re-layouts: 27.6 us -> 2.65 us
  other arithmetic: 15.1 us -> 39.3 us
  between operations: 14.7 us -> 0.98 us
    pallas_call x0 -> x3, Pallas kernels: none -> 102 us  [the longest x1 54.1 us: shards(): pl.pallas_call(functools.partial(second_kernel, nb, ns), out_shape=(f32(n...]
    unnamed x3 -> x0, waiting for transfers between devices: 57.4 us -> none
    all_to_all x4 -> x0, waiting for transfers between devices: 51 us -> none  [the longest x1 29.4 us: shards(): lax.all_to_all(plane_real, 'band', split_axis=2, concat_axis=1, tiled=True)]
    psum x1 -> x0, waiting for transfers between devices: 46 us -> none  [shards(): total_real, total_imag = lax.psum((spec_real, spec_imag), 'spin')]
    psum x1 -> x0, blocking collectives: 39.3 us -> none  [shards(): stress = lax.psum(partial_stress, ('band', 'spin'))]
    dot_general x14 -> x8, matrix products: 47.6 us -> 8.48 us  [the longest x2 2.96 us: shards(): planes.append(jnp.dot(along, table.astype(np.float32), precision=high))]
    all_to_all x4 -> x0, starting transfers between devices: 28.9 us -> none  [the longest x1 7.95 us: shards(): lax.all_to_all(density, 'band', split_axis=2, concat_axis=1, tiled=True)]
    reduce_sum x4 -> x6, other arithmetic: 9.38 us -> 28.7 us  [the longest x1 21.9 us: shards(): jnp.sum(weights[:, None] * (piece[0] * piece[0] + piece[1] * piece[1]), a...]
  transfers between devices with their start and end apart: 6 -> 0, of which waited for: 4 -> 0; matrix products, arithmetic and copies ran while one was open for 21% -> 0% of each run, Pallas kernels for 0% -> 0%
where the time goes in v1:
time: 153 us
  Pallas kernels  102 us (67%)
  other arithmetic  39.3 us (26%)
  matrix products  8.48 us (6%)
  local copies, waits for them, and re-layouts  2.65 us (2%)
    pallas_call x1, Pallas kernels, shards(): pl.pallas_call(functools.partial(second_kernel, nb, ns), out_shape=(f32(n...  54.1 us
    pallas_call x1, Pallas kernels, shards(): pl.pallas_call(functools.partial(first_kernel, nb, ns, fold_y, fold_z), o...  38.6 us
    reduce_sum x1, other arithmetic, shards(): jnp.sum(weights[:, None] * (piece[0] * piece[0] + piece[1] * piece[1]), a...  21.9 us
    pallas_call x1, Pallas kernels, shards(): pl.pallas_call(functools.partial(third_kernel, nb, ns), out_shape=f32(8,...  8.86 us
    convert_element_type x1, other arithmetic, shards(): piece = coefficients[0].astype(jnp.float32)  4.73 us
    squeeze x1, other arithmetic, shards(): factor = jnp.concatenate([factor[0], factor[1]], axis=2)  4.33 us
    reduce_sum x3, other arithmetic, six_rows(): return jnp.stack([jnp.sum(t, axis=dims) for t in terms])  3.38 us

profile of v1, /device:TPU:0, one launch (start us, length us, event | category | flops | bytes accessed | tf_op | source)
XLA Modules:
  0.0 153.0 jit_solution(17237286597526527281)
XLA Ops:
  0.6 0.0 copy-start.13
  0.6 4.7 %convert_element_type.16 = f32[1,2,2,524288]{3,2,1,0:T(2,128)S(1)} convert(bf16[1,2,2,524288]{3,2,1,0:T(2,128)(2,1)} %param.19) | non-fusion elementwise | flops 2097152 | bytes 12582912 | tf_op jit(solution)/shard_map/convert_element_type | solution.py:259
  5.4 0.0 copy-done.13
  5.4 0.0 copy-start
  5.4 0.0 copy-start.6
  5.4 21.9 %fusion.3 = f32[524288]{0:T(1024)S(1)} fusion(f32[1,2,2,524288]{3,2,1,0:T(2,128)S(1)} %convert_element_type.16, f32[2]{0:T(128)S(1)} %multiply_bitcast_fusion.1), kind=kLoop, calls=%fused_computation.5 | loop fusion | flops 4718592 | bytes 10485768 | tf_op jit(solution)/shard_map/reduce_sum | solution.py:260
  27.4 0.0 copy-start.5
  27.4 0.0 copy-done
  27.4 38.6 %first_exchange.1 = (f32[16,16,8,128]{3,2,1,0:T(8,128)S(1)}, f32[1,8,16,8,128]{4,3,2,1,0:T(8,128)S(1)}, f32[128,128]{1,0:T(8,128)S(1)}) custom-call(f32[16,16,8,128]{3,2,1,0:T(8,128)S(1)} %bitcast.129, f32[4,2,2,2,128,128]{5,4,3,2,1,0:T(8,128)S(1)} %bitcast.130), custom_call_target="tpu_custom_call" | custom-call | tf_op jit(solution)/shard_map/first_exchange/pallas_call | solution.py:264
  66.0 0.0 copy-done.6
  66.0 0.6 convolution_bitcast_fusion.6
  66.6 0.0 copy-done.5
  66.6 0.6 convolution_bitcast_fusion.7
  67.2 1.0 pad_maximum_fusion
  68.2 1.6 %copy.27 = f32[8,128,256]{2,1,0:T(8,128)S(1)} copy(f32[8,128,256]{1,2,0:T(8,128)} %pad_maximum_fusion) | data formatting | bytes 2097152 | tf_op jit(solution)/shard_map/concatenate | solution.py:287
  69.8 1.5 convolution_bitcast_fusion.4
  71.3 1.5 convolution_bitcast_fusion.5
  72.8 0.0 copy-start.4
  72.8 0.1 pad_maximum_fusion.1.spec
  72.9 0.7 convolution_bitcast_fusion.1
  73.7 0.2 copy.33
  73.9 54.1 %second_exchange.1 = (f32[16,2,8,8,128]{4,3,2,1,0:T(8,128)S(1)}, f32[16,16,8,128]{3,2,1,0:T(8,128)S(1)}) custom-call(f32[2,8,16,8,128]{4,3,2,1,0:T(8,128)S(1)} %pad_maximum_fusion.1.spec, f32[16,16,8,128]{3,2,1,0:T(8,128)S(1)} %bitcast.131), custom_call_target="tpu_custom_call" | custom-call | tf_op jit(solution)/shard_map/second_exchange/pallas_call | solution.py:304
  128.0 0.6 convolution_bitcast_fusion.3
  128.6 1.9 %fusion.9 = (f32[16,128,128]{2,1,0:T(8,128)S(1)}, f32[16,128,128]{2,1,0:T(8,128)S(1)}) fusion(f32[1,16,128,128]{3,2,1,0:T(8,128)S(1)} %copy-done, f32[16,16,8,128]{3,2,1,0:T(8,128)S(1)} %get-tuple-element.11, f32[16,128,128]{2,1,0:T(8,128)S(1)} %convolution_bitcast_fusion.3, f32[128,128,1]{1,0,2:T(8,128)S(1)} %copy-done.4), kind=kOutput, calls=%fused_computation.24 | convolution fusion | flops 204210176 | bytes 5308416 | tf_op jit(solution)/shard_map/ik,zxk->zxi/dot_general | solution.py:324
  130.5 0.0 copy-start.1
  130.6 1.7 %multiply_reduce_fusion.6 = (f32[128]{0:T(128)S(1)}, f32[128]{0:T(128)S(1)}, f32[128]{0:T(128)S(1)}, f32[128]{0:T(128)S(1)}, f32[128]{0:T(128)S(1)}, /*index=5*/f32[128]{0:T(128)S(1)}, f32[1,16,128,128]{3,2,1,0:T(8,128)}) fusion(f32[16,128,128]{2,1,0:T(8,128)S(1)} %get-tuple-element.49, f32[16,128,128]{2,1,0:T(8,128)S(1)} %get-tuple-element.48, ...), kind=kLoop, calls=%fused_computation.59 | loop fusion | flops 5242112 | bytes 5245952 | tf_op jit(solution)/shard_map/reduce_sum | solution.py:51
  132.2 1.1 convolution_bitcast_fusion
  133.3 0.5 copy.35
  133.8 0.0 copy-start.12
  133.8 0.0 copy-start.9
  133.9 4.3 %dynamic-slice_bitcast_fusion.1 = (f32[256,8,64]{2,1,0:T(8,128)S(1)}, f32[256,8,64]{2,1,0:T(8,128)}, f32[256,8,64]{2,1,0:T(8,128)}, f32[256,8,64]{2,1,0:T(8,128)}) fusion(f32[2,256,8,128]{3,2,1,0:T(8,128)} %param.23, s32[]{:T(128)S(6)} %select_n.19, s32[]{:T(128)S(6)} %add.118, f32[2,256,8,128]{3,2,1,0:T(8,128)S(1)} %bitcast.134), kind=kLoop, calls=%fused_computation.32 | loop fusion | flops 262144 | bytes 5242888 | tf_op jit(solution)/shard_map/squeeze | solution.py:337
  138.2 0.0 copy-start.10
  138.2 0.0 copy-start.11
  138.2 0.0 copy-done.12
  138.2 0.1 dynamic_slice.17
  138.3 0.1 pad_maximum_fusion.3
  138.4 0.1 fusion.33
  138.5 0.1 broadcast_add_fusion
  138.5 2.7 %fusion.26 = (f32[128]{0:T(128)S(1)}, f32[256,8,128]{2,1,0:T(8,128)S(1)}) fusion(f32[256]{0:T(256)S(1)} %copy-done.9, f32[8,128]{1,0:T(8,128)S(1)} %broadcast_add_fusion, f32[256,8,64]{2,1,0:T(8,128)} %get-tuple-element.50, f32[256,8,64]{2,1,0:T(8,128)} %get-tuple-element.51, f32[256,8,64]{2,1,0:T(8,128)} %get-tuple-element.37, ...), kind=kLoop, calls=%fused_computation.62 | loop fusion | flops 3669888 | bytes 3151360 | tf_op jit(solution)/shard_map/reduce_sum | solution.py:349
  141.3 0.0 copy-done.7
  141.3 0.0 copy-done.8
  141.3 1.0 multiply_reduce_fusion.1
  142.4 0.1 add_multiply_fusion
  142.5 0.1 fusion.32
  142.7 0.7 multiply_reduce_fusion.9
  143.4 0.1 subtract_add_fusion
  143.5 8.9 %stress_sum.1 = f32[8,128]{1,0:T(8,128)S(1)} custom-call(f32[8,128]{1,0:T(8,128)S(1)} %concatenate.24.part), custom_call_target="tpu_custom_call" | custom-call | tf_op jit(solution)/shard_map/stress_sum/pallas_call | solution.py:352
  152.3 0.6 slice_reduce_fusion
  (16 shorter events, 0.1 us)
Async XLA Ops:
  0.6 4.8 %copy-start.13 = (s32[1,2]{1,0:T(1,128)S(1)}, s32[1,2]{1,0:T(1,128)}, u32[]{:S(2)}) copy-start(s32[1,2]{1,0:T(1,128)} %param.20) | copy-start | bytes 28
  5.4 22.0 %copy-start = (f32[1,16,128,128]{3,2,1,0:T(8,128)S(1)}, f32[1,16,128,128]{3,2,1,0:T(8,128)}, u32[]{:S(2)}) copy-start(f32[1,16,128,128]{3,2,1,0:T(8,128)} %param.22) | copy-start | bytes 3145732
  5.4 60.5 %copy-start.6 = (f32[128,128,1]{1,0,2:T(8,128)S(1)}, f32[128,128,1]{1,0,2:T(8,128)}, u32[]{:S(2)}) copy-start(f32[128,128,1]{1,0,2:T(8,128)} %constant.96) | copy-start | bytes 196612
  27.4 39.2 %copy-start.5 = (f32[128,128,1]{1,0,2:T(8,128)S(1)}, f32[128,128,1]{1,0,2:T(8,128)}, u32[]{:S(2)}) copy-start(f32[128,128,1]{1,0,2:T(8,128)} %constant.95) | copy-start | bytes 196612
  68.2 4.7 %copy-start.2 = (f32[256,256]{1,0:T(8,128)S(1)}, f32[256,256]{1,0:T(8,128)}, u32[]{:S(2)}) copy-start(f32[256,256]{1,0:T(8,128)} %constant.76.clone) | copy-start | bytes 786436
  72.8 55.2 %copy-start.4 = (f32[128,128,1]{1,0,2:T(8,128)S(1)}, f32[128,128,1]{1,0,2:T(8,128)}, u32[]{:S(2)}) copy-start(f32[128,128,1]{1,0,2:T(8,128)} %constant.94) | copy-start | bytes 196612
  130.5 1.7 %copy-start.1 = (f32[512,256]{1,0:T(8,128)S(1)}, f32[512,256]{1,0:T(8,128)}, u32[]{:S(2)}) copy-start(f32[512,256]{1,0:T(8,128)} %constant.79.clone) | copy-start | bytes 1572868
  133.8 4.4 %copy-start.12 = (f32[128]{0:T(128)S(1)}, f32[128]{0:T(128)}, u32[]{:S(2)}) copy-start(f32[128]{0:T(128)} %constant.80.clone) | copy-start | bytes 1540
  133.8 4.7 %copy-start.9 = (f32[256]{0:T(256)S(1)}, f32[256]{0:T(256)}, u32[]{:S(2)}) copy-start(f32[256]{0:T(256)} %constant.90) | copy-start | bytes 3076
  138.2 3.1 %copy-start.7 = (f32[256]{0:T(256)S(1)}, f32[256]{0:T(256)}, u32[]{:S(2)}) copy-start(f32[256]{0:T(256)} %constant.91) | copy-start | bytes 3076
  138.2 3.1 %copy-start.8 = (f32[256]{0:T(256)S(1)}, f32[256]{0:T(256)}, u32[]{:S(2)}) copy-start(f32[256]{0:T(256)} %constant.92) | copy-start | bytes 3076
  138.2 4.2 %copy-start.3 = (s32[3,16384]{1,0:T(4,128)S(1)}, s32[3,16384]{1,0:T(4,128)}, u32[]{:S(2)}) copy-start(s32[3,16384]{1,0:T(4,128)} %param.21) | copy-start | bytes 589828
  138.2 4.2 %copy-start.10 = (f32[3]{0:T(128)S(1)}, f32[3]{0:T(128)}, u32[]{:S(2)}) copy-start(f32[3]{0:T(128)} %constant.77.clone) | copy-start | bytes 40
  138.2 5.2 %copy-start.11 = (f32[6]{0:T(128)S(1)}, f32[6]{0:T(128)}, u32[]{:S(2)}) copy-start(f32[6]{0:T(128)} %constant.93) | copy-start | bytes 76

commit v2 on v1

--- a/solution.py
+++ b/solution.py
@@ -73,50 +73,89 @@
     return 1 + (k + count // 2 - 1) % (count - 1)
 
 
-def first_kernel(
-    nb, ns, ny, nz, dens, kin, dcol, half, kout,
-    from_core, sum_core, from_plane, sum_plane, from_line,
+def split(value):
+    high = value.astype(jnp.bfloat16)
+    return high, (value - high.astype(jnp.float32)).astype(jnp.bfloat16)
+
+
+def host_split(table):
+    high = table.astype(np.float32).astype(jnp.bfloat16)
+    low = (table - high.astype(np.float64)).astype(np.float32).astype(jnp.bfloat16)
+    return np.stack([high, low])
+
+
+def dot3(left, right):
+    def one(p, q):
+        return jnp.dot(p, q, preferred_element_type=jnp.float32)
+
+    return one(left[0], right[0]) + (one(left[0], right[1]) + one(left[1], right[0]))
+
+
+def loop(low, high, step):
+    def body(k, carry):
+        step(k)
+        return carry
+
+    lax.fori_loop(low, high, body, 0)
+
+
+def main_kernel(
+    nb, ns, ny, nz, dens, coef, weight, pairs, table_x, table_y, table_d,
+    scol, gout, kout,
+    kin, dcol, half, spec, grad, from_core, sum_core, from_plane, sum_plane, from_line,
     d_send, d_recv, h_send, h_recv, c_send, c_recv, p_send, p_recv, l_send, l_recv,
+    s_send, s_recv, g_send, g_recv,
 ):
     b, s = greet_all(nb, ns)
+    n = nb * ns
     core, y, z = b % 2, (b // 2) % ny, b // (2 * ny)
-    zh = dens.shape[0] // ns
-
-    core_copy = pltpu.make_async_remote_copy(
-        kin.at[:, :, 1 - core], from_core, c_send.at[0], c_recv.at[0],
-        device_id=(b + 1 - 2 * core, s), device_id_type=MESH,
-    )
-    core_copy.start()
+    zl, _, xl, width = dens.shape
+    zh = zl // ns
+    nx = nb * xl
+    rows = kout.shape[0]
 
     half_copies = []
     for k in range(1, ns):
         other = (s + k) % ns
-        half_copies.append(
-            pltpu.make_async_remote_copy(
-                dens.at[pl.ds(other * zh, zh)], half.at[k - 1], h_send.at[k - 1], h_recv.at[k - 1],
-                device_id=(b, other), device_id_type=MESH,
-            )
-        )
+        copy = pltpu.make_async_remote_copy(
+            dens.at[pl.ds(other * zh, zh)], half.at[k - 1], h_send.at[k - 1], h_recv.at[k - 1],
+            device_id=(b, other), device_id_type=MESH,
+        )
+        copy.start()
+        half_copies.append(copy)
 
     def column_copy(k):
-        offset = far_first(k, nb)
-        to = (b + offset) % nb
+        to = (b + far_first(k, nb)) % nb
         return pltpu.make_async_remote_copy(
             dens.at[:, to], dcol.at[b], d_send.at[k], d_recv.at[k],
             device_id=(to, s), device_id_type=MESH,
         )
 
-    def start_column(k, carry):
-        column_copy(k).start()
-        return carry
-
-    lax.fori_loop(0, nb - 1, start_column, 0)
-    for copy in half_copies:
-        copy.start()
+    loop(0, nb - 1, lambda k: column_copy(k).start())
     dcol[b] = dens[:, b]
 
+    depth = weight.shape[0]
+
+    def kinetic(i):
+        here = pl.ds(pl.multiple_of(i * depth, depth), depth)
+        real, imag = coef[0, here, :].astype(jnp.float32), coef[1, here, :].astype(jnp.float32)
+        high, low = split(weight[...] * (real * real + imag * imag))
+        kin[i // (2 * ns), (i // ns) % 2, i % ns] = jnp.dot(
+            pairs[...], high, preferred_element_type=jnp.float32
+        ) + jnp.dot(pairs[...], low, preferred_element_type=jnp.float32)
+
+    loop(0, n, kinetic)
+    core_copy = pltpu.make_async_remote_copy(
+        kin.at[:, 1 - core], from_core, c_send.at[0], c_recv.at[0],
+        device_id=(b + 1 - 2 * core, s), device_id_type=MESH,
+    )
+    core_copy.start()
     core_copy.wait()
-    sum_core[...] = kin[:, :, core] + from_core[...]
+
+    def add_core(i):
+        sum_core[i // ny, i % ny] = kin[i, core] + from_core[i]
+
+    loop(0, nz * ny, add_core)
     plane_copies = []
     for k in range(1, ny * ns):
         ty, ts = (y + k // ns) % ny, (s + k % ns) % ns
@@ -126,6 +165,47 @@
         )
         copy.start()
         plane_copies.append(copy)
+
+    for copy in half_copies:
+        copy.wait()
+
+    def plane(i):
+        total = dens[s * zh + i]
+        for k in range(ns - 1):
+            total = total + half[k, i]
+        along = dot3((table_x[0], table_x[1]), split(total.reshape(nx, width)))
+        both = split(jnp.concatenate([along[:nx], along[nx:]], axis=1))
+        for k in range(ns):
+            spec[k, i] = dot3(both, (table_y[0, k], table_y[1, k])).reshape(nb, xl, -1)
+
+    loop(0, zh, plane)
+
+    def spec_copy(k):
+        offset = far_first(k, n)
+        tb, ts = (b + offset // ns) % nb, (s + offset % ns) % ns
+        return pltpu.make_async_remote_copy(
+            spec.at[ts, :, tb], scol.at[b, s], s_send.at[k], s_recv.at[k],
+            device_id=(tb, ts), device_id_type=MESH,
+        )
+
+    loop(0, n - 1, lambda k: spec_copy(k).start())
+    scol[b, s] = spec[s, :, b]
+
+    loop(0, nb - 1, lambda k: column_copy(k).wait())
+    for x in range(xl):
+        column = split(dcol[:, :, x, :].reshape(nb * zl, width))
+        grad[:, :, x, :] = dot3((table_d[0], table_d[1]), column).reshape(nb, zl, width)
+
+    def grad_copy(k):
+        to = (b + far_first(k, nb)) % nb
+        return pltpu.make_async_remote_copy(
+            grad.at[to], gout.at[:, b], g_send.at[k], g_recv.at[k],
+            device_id=(to, s), device_id_type=MESH,
+        )
+
+    loop(0, nb - 1, lambda k: grad_copy(k).start())
+    gout[:, b] = grad[b]
+
     for copy in plane_copies:
         copy.wait()
     total = sum_core[:, y, s]
@@ -140,70 +220,11 @@
             device_id=((tz * ny + y) * 2 + core, s), device_id_type=MESH,
         )
 
-    def start_line(k, carry):
-        line_copy(k).start()
-        return carry
-
-    def wait_line(k, carry):
-        line_copy(k).wait()
-        return carry
-
-    lax.fori_loop(1, nz, start_line, 0)
-    lax.fori_loop(1, nz, wait_line, 0)
+    loop(1, nz, lambda k: line_copy(k).start())
+    loop(1, nz, lambda k: line_copy(k).wait())
     kout[...] = sum_plane[z] + jnp.sum(from_line[...], axis=0)
-
-    for copy in half_copies:
-        copy.wait()
-
-    def wait_column(k, carry):
-        column_copy(k).wait()
-        return carry
-
-    lax.fori_loop(0, nb - 1, wait_column, 0)
-
-
-def second_kernel(nb, ns, spec, grad, scol, gout, s_send, s_recv, g_send, g_recv):
-    b, s = greet_all(nb, ns)
-    n = nb * ns
-
-    def spec_copy(k):
-        offset = far_first(k, n)
-        tb, ts = (b + offset // ns) % nb, (s + offset % ns) % ns
-        return pltpu.make_async_remote_copy(
-            spec.at[ts, :, tb], scol.at[b, s], s_send.at[k], s_recv.at[k],
-            device_id=(tb, ts), device_id_type=MESH,
-        )
-
-    def grad_copy(k):
-        to = (b + far_first(k, nb)) % nb
-        return pltpu.make_async_remote_copy(
-            grad.at[to], gout.at[:, b], g_send.at[k], g_recv.at[k],
-            device_id=(to, s), device_id_type=MESH,
-        )
-
-    def start_grad(k, carry):
-        grad_copy(k).start()
-        return carry
-
-    def start_spec(k, carry):
-        spec_copy(k).start()
-        return carry
-
-    lax.fori_loop(0, nb - 1, start_grad, 0)
-    lax.fori_loop(0, n - 1, start_spec, 0)
-    gout[:, b] = grad[b]
-    scol[b, s] = spec[s, :, b]
-
-    def wait_grad(k, carry):
-        grad_copy(k).wait()
-        return carry
-
-    def wait_spec(k, carry):
-        spec_copy(k).wait()
-        return carry
-
-    lax.fori_loop(0, nb - 1, wait_grad, 0)
-    lax.fori_loop(0, n - 1, wait_spec, 0)
+    loop(0, n - 1, lambda k: spec_copy(k).wait())
+    loop(0, nb - 1, lambda k: grad_copy(k).wait())
 
 
 def third_kernel(nb, ns, part, out, held, send, recv):
@@ -256,62 +277,58 @@
     b, s = lax.axis_index("band"), lax.axis_index("spin")
 
     weights = occupation[0].astype(jnp.float32) / occupation_unit
-    piece = coefficients[0].astype(jnp.float32)
-    kin = jnp.sum(weights[:, None] * (piece[0] * piece[0] + piece[1] * piece[1]), axis=0)
-    kin = kin.reshape(fold_z, fold_y, 2, ns, rows, 128)
+    nbl = coefficients.shape[2]
+    depth = rows * nbl
+    coef = coefficients[0].reshape(2, nbl, npw // 128, 128)
+    coef = coef.transpose(0, 2, 1, 3).reshape(2, npw // 128 * nbl, 128)
+    weight = jnp.broadcast_to(jnp.tile(weights, rows)[:, None], (depth, 128))
+    pairs = jnp.asarray(np.kron(np.eye(rows), np.ones((1, nbl))), jnp.bfloat16)
     dens = density[0]
-
-    dcol, half, kinetic_weight = pl.pallas_call(
-        functools.partial(first_kernel, nb, ns, fold_y, fold_z),
-        out_shape=(f32(nb, zl, xl, ny), f32(ns - 1, zh, nb, xl, ny), f32(rows, 128)),
-        in_specs=[VMEM] * 2,
-        out_specs=(VMEM,) * 3,
-        scratch_shapes=[
-            pltpu.VMEM((fold_z, fold_y, ns, rows, 128), jnp.float32),
-            pltpu.VMEM((fold_z, fold_y, ns, rows, 128), jnp.float32),
-            pltpu.VMEM((fold_y * ns - 1, fold_z, rows, 128), jnp.float32),
-            pltpu.VMEM((fold_z, rows, 128), jnp.float32),
-            pltpu.VMEM((fold_z - 1, rows, 128), jnp.float32),
-            dma((nb - 1,)), dma((nb - 1,)), dma((ns - 1,)), dma((ns - 1,)), dma((1,)), dma((1,)),
-            dma((fold_y * ns - 1,)), dma((fold_y * ns - 1,)), dma((fold_z - 1,)), dma((fold_z - 1,)),
-        ],
-        compiler_params=params(0),
-        name="first_exchange",
-    )(dens.reshape(zl, nb, xl, ny), kin)
-
-    own = lax.dynamic_slice_in_dim(dens, s * zh, zh, 0)
-    total = own + jnp.sum(half, axis=0).reshape(zh, nx, ny)
     cos_x, sin_x = fourier_tables(nx)
     cos_y, sin_y = fourier_tables(ny)
     cos_z, sin_z = fourier_tables(nzg)
-    along = jnp.concatenate(
-        [
-            jnp.einsum("mj,zjy->zmy", cos_x.astype(np.float32), total, precision=high),
-            jnp.einsum("mj,zjy->zmy", (-sin_x).astype(np.float32), total, precision=high),
-        ],
-        axis=2,
-    ).reshape(zh * nx, 2 * ny)
     part = ny // ns
-    planes = []
+    table_y = []
     for k in range(ns):
         cut = slice(k * part, (k + 1) * part)
-        table = np.block([[cos_y[:, cut], -sin_y[:, cut]], [sin_y[:, cut], cos_y[:, cut]]])
-        planes.append(jnp.dot(along, table.astype(np.float32), precision=high))
-    spec = jnp.stack(planes).reshape(ns, zh, nb, xl, lanes)
-
-    grad_col = jnp.dot(derivative_table(nzg), dcol.reshape(nzg, xl * ny), precision=high)
-
-    scol, gout = pl.pallas_call(
-        functools.partial(second_kernel, nb, ns),
-        out_shape=(f32(nb, ns, zh, xl, lanes), f32(zl, nb, xl, ny)),
-        in_specs=[VMEM] * 2,
-        out_specs=(VMEM,) * 2,
+        table_y.append(np.block([[cos_y[:, cut], -sin_y[:, cut]], [sin_y[:, cut], cos_y[:, cut]]]))
+
+    scol, gout, kinetic_weight = pl.pallas_call(
+        functools.partial(main_kernel, nb, ns, fold_y, fold_z),
+        out_shape=(f32(nb, ns, zh, xl, lanes), f32(zl, nb, xl, ny), f32(rows, 128)),
+        in_specs=[VMEM] * 7,
+        out_specs=(VMEM,) * 3,
         scratch_shapes=[
-            dma((nb * ns - 1,)), dma((nb * ns - 1,)), dma((nb - 1,)), dma((nb - 1,)),
+            pltpu.VMEM(shape, jnp.float32)
+            for shape in (
+                (fold_z * fold_y, 2, ns, rows, 128),
+                (nb, zl, xl, ny),
+                (ns - 1, zh, nb, xl, ny),
+                (ns, zh, nb, xl, lanes),
+                (nb, zl, xl, ny),
+                (fold_z * fold_y, ns, rows, 128),
+                (fold_z, fold_y, ns, rows, 128),
+                (fold_y * ns - 1, fold_z, rows, 128),
+                (fold_z, rows, 128),
+                (fold_z - 1, rows, 128),
+            )
+        ]
+        + [
+            dma((count,))
+            for length in (nb - 1, ns - 1, 1, fold_y * ns - 1, fold_z - 1, nb * ns - 1, nb - 1)
+            for count in (length, length)
         ],
-        compiler_params=params(1),
-        name="second_exchange",
-    )(spec, grad_col.reshape(nb, zl, xl, ny))
+        compiler_params=params(0),
+        name="main_exchange",
+    )(
+        dens.reshape(zl, nb, xl, ny),
+        coef,
+        weight,
+        pairs,
+        host_split(np.concatenate([cos_x, -sin_x])),
+        host_split(np.stack(table_y)),
+        host_split(derivative_table(nzg).astype(np.float64)),
+    )
 
     gvec = spacing * (miller.astype(jnp.float32) + jnp.array(kpoint, jnp.float32)[:, None])
     gvec = gvec.reshape(3, rows, 128)

time: 153 us -> 115 us (0.75)
  other arithmetic: 39.3 us -> 9.48 us
  Pallas kernels: 102 us -> 92.1 us
  local copies, waits for them, and re-layouts: 2.65 us -> 8.78 us
  matrix products: 8.48 us -> 3.6 us
    reduce_sum x1 -> x0, other arithmetic: 21.9 us -> none  [shards(): jnp.sum(weights[:, None] * (piece[0] * piece[0] + piece[1] * piece[1]), a...]
    pallas_call x2 -> x1, Pallas kernels: 92.7 us -> 82.8 us  [shards(): pl.pallas_call(functools.partial(main_kernel, nb, ns, fold_y, fold_z), ou...]
    unnamed x30 -> x31, local copies, waits for them, and re-layouts: 0.75 us -> 7.58 us
    dot_general x5 -> x0, matrix products: 4.88 us -> none  [the longest x2 2.96 us: shards(): planes.append(jnp.dot(along, table.astype(np.float32), precision=high))]
    convert_element_type x1 -> x0, other arithmetic: 4.73 us -> none  [shards(): piece = coefficients[0].astype(jnp.float32)]
    reduce_sum x1, other arithmetic: 2.74 us -> 0.88 us  [shards(): spec_rows = spec_rows - diagonal * jnp.sum(hartree, axis=(0, 1))[None]]
    squeeze x1, other arithmetic: 4.33 us -> 2.69 us  [shards(): factor = jnp.concatenate([factor[0], factor[1]], axis=2)]
    concatenate x1 -> x0, local copies, waits for them, and re-layouts: 1.6 us -> none  [shards(): jnp.concatenate([jnp.einsum('mj,zjy->zmy', cos_x.astype(np.float32), tota...]
where the time goes in v2:
time: 115 us
  Pallas kernels  92.1 us (80%)
  other arithmetic  9.48 us (8%)
  local copies, waits for them, and re-layouts  8.78 us (8%)
  matrix products  3.6 us (3%)
    pallas_call x1, Pallas kernels, shards(): pl.pallas_call(functools.partial(main_kernel, nb, ns, fold_y, fold_z), ou...  82.8 us
    pallas_call x1, Pallas kernels, shards(): pl.pallas_call(functools.partial(third_kernel, nb, ns), out_shape=f32(8,...  9.23 us
    unnamed x31, local copies, waits for them, and re-layouts  7.58 us
    reduce_sum x3, other arithmetic, six_rows(): return jnp.stack([jnp.sum(t, axis=dims) for t in terms])  3.56 us
    squeeze x1, other arithmetic, shards(): factor = jnp.concatenate([factor[0], factor[1]], axis=2)  2.69 us

profile of v2, /device:TPU:0, one launch (start us, length us, event | category | flops | bytes accessed | tf_op | source)
XLA Modules:
  0.0 114.8 jit_solution(9485013901558190137)
XLA Ops:
  0.6 0.7 dynamic_slice.10
  1.4 0.1 pad_maximum_fusion.1
  1.4 0.7 fusion.23
  2.2 0.1 broadcast_add_fusion
  2.3 0.7 multiply_bitcast_fusion.1
  2.9 0.1 broadcast_in_dim.9
  3.1 0.1 broadcast_in_dim.10.weight
  3.2 0.0 copy-start
  3.2 2.2 %copy-done = bf16[1,2,2,524288]{3,2,1,0:T(2,128)(2,1)S(1)} copy-done((bf16[1,2,2,524288]{3,2,1,0:T(2,128)(2,1)S(1)}, bf16[1,2,2,524288]{3,2,1,0:T(2,128)(2,1)}, u32[]{:S(2)}) %copy-start) | copy-done | bytes 4194328
  5.4 0.0 copy-start.1
  5.4 1.2 %copy-done.1 = f32[1,16,128,128]{3,2,1,0:T(8,128)S(1)} copy-done((f32[1,16,128,128]{3,2,1,0:T(8,128)S(1)}, f32[1,16,128,128]{3,2,1,0:T(8,128)}, u32[]{:S(2)}) %copy-start.1) | copy-done | bytes 1048600
  6.6 0.9 copy-done.3
  7.5 0.0 copy-start.4
  7.5 0.9 copy-done.4
  8.5 0.9 copy-done.5
  9.4 0.8 copy-done.6
  10.2 82.8 %main_exchange.1 = (f32[16,2,8,8,128]{4,3,2,1,0:T(8,128)S(1)}, f32[16,16,8,128]{3,2,1,0:T(8,128)S(1)}, f32[128,128]{1,0:T(8,128)S(1)}) custom-call(f32[16,16,8,128]{3,2,1,0:T(8,128)S(1)} %bitcast.85, bf16[2,8192,128]{2,1,0:T(8,128)(2,1)S(1)} %bitcast.84, f32[256,128]{1,0:T(8,128)S(1)} %broadcast_in_dim.10.weight, bf16[128,256]{1,0:T(8,128)(2,1)S(1)} %copy-done.6, ...), custom_call_target="tpu_custom_call" | custom-call | tf_op jit(solution)/shard_map/main_exchange/pallas_call | solution.py:296
  93.1 0.0 copy-done.7
  93.1 1.1 convolution_bitcast_fusion
  94.2 0.5 copy.24
  94.6 0.0 copy-start.12
  94.7 2.7 %dynamic-slice_bitcast_fusion.1 = (f32[256,8,64]{2,1,0:T(8,128)S(1)}, f32[256,8,64]{2,1,0:T(8,128)S(1)}, f32[256,8,64]{2,1,0:T(8,128)S(1)}, f32[256,8,64]{2,1,0:T(8,128)S(1)}) fusion(f32[2,256,8,128]{3,2,1,0:T(8,128)} %param.22, s32[]{:T(128)S(6)} %select_n.15, s32[]{:T(128)S(6)} %add.101, f32[2,256,8,128]{3,2,1,0:T(8,128)S(1)} %bitcast.87), kind=kLoop, calls=%fused_computation.19 | loop fusion | flops 262144 | bytes 5242888 | tf_op jit(solution)/shard_map/squeeze | solution.py:354
  97.4 0.0 copy-done.12
  97.4 0.0 copy-start.10
  97.4 0.0 copy-start.11
  97.4 0.0 copy-start.2
  97.4 0.0 copy-start.9
  97.4 0.9 fusion.18
  98.3 0.0 copy-done.10
  98.3 0.0 copy-done.11
  98.3 1.2 %multiply_reduce_fusion.1 = (f32[128]{0:T(128)S(1)}, f32[128]{0:T(128)S(1)}, f32[128]{0:T(128)S(1)}, f32[128]{0:T(128)S(1)}, f32[128]{0:T(128)S(1)}, /*index=5*/f32[128]{0:T(128)S(1)}) fusion(f32[256,8,128]{2,1,0:T(8,128)S(1)} %get-tuple-element.29, f32[256]{0:T(256)S(1)} %copy-done.10, f32[8]{0:T(128)S(1)} %get-tuple-element.40, ...), kind=kLoop, calls=%fused_computation.37 | loop fusion | flops 3931392 | bytes 1054784 | tf_op jit(solution)/shard_map/reduce_sum | solution.py:51
  99.6 0.0 copy-done.2
  99.6 0.0 copy-done.9
  99.6 0.6 convolution_bitcast_fusion.2
  100.2 1.9 %fusion.5 = (f32[16,128,128]{2,1,0:T(8,128)S(1)}, f32[16,128,128]{2,1,0:T(8,128)S(1)}) fusion(f32[1,16,128,128]{3,2,1,0:T(8,128)S(1)} %copy-done.2, f32[16,16,8,128]{3,2,1,0:T(8,128)S(1)} %get-tuple-element.7, f32[16,128,128]{2,1,0:T(8,128)S(1)} %convolution_bitcast_fusion.2, f32[128,128,1]{1,0,2:T(8,128)S(1)} %copy-done.9), kind=kOutput, calls=%fused_computation.13 | convolution fusion | flops 204210176 | bytes 5308416 | tf_op jit(solution)/shard_map/ik,zxk->zxi/dot_general | solution.py:341
  102.1 0.0 copy-start.8
  102.1 0.0 copy-start.13
  102.1 0.0 copy-start.14
  102.2 1.7 %multiply_reduce_fusion.6 = (f32[128]{0:T(128)S(1)}, f32[128]{0:T(128)S(1)}, f32[128]{0:T(128)S(1)}, f32[128]{0:T(128)S(1)}, f32[128]{0:T(128)S(1)}, /*index=5*/f32[128]{0:T(128)S(1)}, f32[1,16,128,128]{3,2,1,0:T(8,128)}) fusion(f32[16,128,128]{2,1,0:T(8,128)S(1)} %get-tuple-element.45, f32[16,128,128]{2,1,0:T(8,128)S(1)} %get-tuple-element.44, ...), kind=kLoop, calls=%fused_computation.42 | loop fusion | flops 5242112 | bytes 5245952 | tf_op jit(solution)/shard_map/reduce_sum | solution.py:51
  103.8 0.0 copy-done.8
  103.8 0.0 copy-done.13
  103.8 0.1 add_multiply_fusion
  104.0 0.1 fusion.22
  104.1 0.7 multiply_reduce_fusion.9
  104.8 0.0 copy-done.14
  104.8 0.1 subtract_add_fusion
  104.9 9.2 %stress_sum.1 = f32[8,128]{1,0:T(8,128)S(1)} custom-call(f32[8,128]{1,0:T(8,128)S(1)} %concatenate.19.part), custom_call_target="tpu_custom_call" | custom-call | tf_op jit(solution)/shard_map/stress_sum/pallas_call | solution.py:369
  114.2 0.6 slice_reduce_fusion
  (9 shorter events, 0.1 us)
Async XLA Ops:
  3.2 2.2 %copy-start = (bf16[1,2,2,524288]{3,2,1,0:T(2,128)(2,1)S(1)}, bf16[1,2,2,524288]{3,2,1,0:T(2,128)(2,1)}, u32[]{:S(2)}) copy-start(bf16[1,2,2,524288]{3,2,1,0:T(2,128)(2,1)} %param.18) | copy-start | bytes 12582916
  5.4 1.2 %copy-start.1 = (f32[1,16,128,128]{3,2,1,0:T(8,128)S(1)}, f32[1,16,128,128]{3,2,1,0:T(8,128)}, u32[]{:S(2)}) copy-start(f32[1,16,128,128]{3,2,1,0:T(8,128)} %param.21) | copy-start | bytes 3145732
  6.6 0.9 copy-start.3
  7.5 0.9 copy-start.4
  8.5 0.9 copy-start.5
  9.4 0.8 copy-start.6
  10.2 82.8 %copy-start.7 = (f32[512,256]{1,0:T(8,128)S(1)}, f32[512,256]{1,0:T(8,128)}, u32[]{:S(2)}) copy-start(f32[512,256]{1,0:T(8,128)} %constant.73.clone) | copy-start | bytes 1572868
  94.6 2.7 %copy-start.12 = (f32[256]{0:T(256)S(1)}, f32[256]{0:T(256)}, u32[]{:S(2)}) copy-start(f32[256]{0:T(256)} %constant.84) | copy-start | bytes 3076
  97.4 0.9 copy-start.10
  97.4 0.9 copy-start.11
  97.4 2.2 %copy-start.2 = (f32[1,16,128,128]{3,2,1,0:T(8,128)S(1)}, f32[1,16,128,128]{3,2,1,0:T(8,128)}, u32[]{:S(2)}) copy-start(f32[1,16,128,128]{3,2,1,0:T(8,128)} %param.21) | copy-start | bytes 3145732
  97.4 2.2 %copy-start.9 = (f32[128,128,1]{1,0,2:T(8,128)S(1)}, f32[128,128,1]{1,0,2:T(8,128)}, u32[]{:S(2)}) copy-start(f32[128,128,1]{1,0,2:T(8,128)} %constant.88) | copy-start | bytes 196612
  102.1 1.7 %copy-start.8 = (s32[3,16384]{1,0:T(4,128)S(1)}, s32[3,16384]{1,0:T(4,128)}, u32[]{:S(2)}) copy-start(s32[3,16384]{1,0:T(4,128)} %param.20) | copy-start | bytes 589828
  102.1 1.7 %copy-start.13 = (f32[3]{0:T(128)S(1)}, f32[3]{0:T(128)}, u32[]{:S(2)}) copy-start(f32[3]{0:T(128)} %constant.71.clone) | copy-start | bytes 40
  102.1 2.7 %copy-start.14 = (f32[6]{0:T(128)S(1)}, f32[6]{0:T(128)}, u32[]{:S(2)}) copy-start(f32[6]{0:T(128)} %constant.87) | copy-start | bytes 76

commit v3 on v2

v3 whole, which is shorter than its diff:
```python
import functools

import jax
import jax.numpy as jnp
import numpy as np
from jax import lax
from jax.experimental import pallas as pl
from jax.experimental.pallas import tpu as pltpu
from jax.sharding import PartitionSpec as P

occupation_unit = 1000.0
kpoint = (0.25, 0.125, 0.375)
spacing = 0.25
MESH = pl.DeviceIdType.MESH
VMEM = pl.BlockSpec(memory_space=pltpu.VMEM)


def derivative_table(length):
    index = np.arange(length)
    wrapped = np.mod(index[:, None] - index[None, :], length)
    angles = np.pi / length * wrapped
    sines = np.where(wrapped == 0, 1.0, np.sin(angles))
    parity = 1.0 - 2.0 * np.mod(wrapped, 2)
    table = np.where(wrapped == 0, 0.0, 0.5 * parity * np.cos(angles) / sines)
    return table.astype(np.float32)


def fourier_tables(length):
    index = np.arange(length)
    phases = np.mod(index[:, None] * index[None, :], length) * (2.0 * np.pi / length)
    return np.cos(phases), np.sin(phases)


def greet_all(nb, ns):
    b, s = lax.axis_index("band"), lax.axis_index("spin")
    barrier = pltpu.get_barrier_semaphore()

    def greet(k, carry):
        pl.semaphore_signal(
            barrier,
            inc=1,
            device_id=((b + k // ns) % nb, (s + k % ns) % ns),
            device_id_type=MESH,
        )
        return carry

    lax.fori_loop(1, nb * ns, greet, 0)
    pl.semaphore_wait(barrier, nb * ns - 1)
    return b, s


def far_first(k, count):
    return 1 + (k + count // 2 - 1) % (count - 1)


def split(value):
    high = value.astype(jnp.bfloat16)
    return high, (value - high.astype(jnp.float32)).astype(jnp.bfloat16)


def host_split(table):
    high = table.astype(np.float32).astype(jnp.bfloat16)
    low = (table - high.astype(np.float64)).astype(np.float32).astype(jnp.bfloat16)
    return np.stack([high, low])


def dot3(left, right):
    def one(p, q):
        return jnp.dot(p, q, preferred_element_type=jnp.float32)

    return one(left[0], right[0]) + (one(left[0], right[1]) + one(left[1], right[0]))


def loop(low, high, step):
    def body(k, carry):
        step(k)
        return carry

    lax.fori_loop(low, high, body, 0)


def axis_frequency(index, length):
    signed = jnp.where(index >= length // 2, index - length, index)
    return 2.0 * np.pi / length * signed.astype(jnp.float32)


def fold(value):
    return jnp.sum(value, axis=0, keepdims=True)


def main_kernel(
    nb, ns, ny, nz, occupation, miller, dens_h, coef_h, factor_h,
    table_x_h, table_y_h, table_d_h, table_z_h, table_g_h, pairs_h,
    stress, kdens, square,
    dens, coef, factor, table_x, table_y, table_d, table_z, table_g, pairs,
    kin, dcol, half, spec, grad, from_core, sum_core, from_plane, sum_plane, from_line,
    scol, gout, grad_x, grad_y, part, held,
    f_sem, d_send, d_recv, h_send, h_recv, c_send, c_recv, p_send, p_recv, l_send, l_recv,
    s_send, s_recv, g_send, g_recv, t_send, t_recv,
):
    sources = (dens_h, coef_h, pairs_h, table_x_h, table_y_h, table_g_h, table_d_h, table_z_h, factor_h)
    targets = (dens, coef, pairs, table_x, table_y, table_g, table_d, table_z, factor)
    fetches = [
        pltpu.make_async_copy(source, target, f_sem.at[i])
        for i, (source, target) in enumerate(zip(sources, targets))
    ]
    for fetch in fetches:
        fetch.start()
    b, s = greet_all(nb, ns)
    n = nb * ns
    core, y, z = b % 2, (b // 2) % ny, b // (2 * ny)
    zl, _, xl, width = dens.shape
    zh = zl // ns
    nx = nb * xl
    nzg = nb * zl
    rows = kdens.shape[0]
    fetches[0].wait()

    half_copies = []
    for k in range(1, ns):
        other = (s + k) % ns
        copy = pltpu.make_async_remote_copy(
            dens.at[pl.ds(other * zh, zh)], half.at[k - 1], h_send.at[k - 1], h_recv.at[k - 1],
            device_id=(b, other), device_id_type=MESH,
        )
        copy.start()
        half_copies.append(copy)

    def column_copy(k):
        to = (b + far_first(k, nb)) % nb
        return pltpu.make_async_remote_copy(
            dens.at[:, to], dcol.at[b], d_send.at[k], d_recv.at[k],
            device_id=(to, s), device_id_type=MESH,
        )

    loop(0, nb - 1, lambda k: column_copy(k).start())
    dcol[b] = dens[:, b]

    nbl = occupation.shape[1]
    depth = rows * nbl
    band = lax.broadcasted_iota(jnp.int32, (depth, 128), 0) % nbl
    weight = jnp.zeros((depth, 128), jnp.float32)
    for j in range(nbl):
        share = jnp.full((depth, 128), occupation[0, j]).astype(jnp.float32) / occupation_unit
        weight = jnp.where(band == j, share, weight)
    for fetch in fetches[1:3]:
        fetch.wait()

    def kinetic(i):
        here = pl.ds(pl.multiple_of(i * depth, depth), depth)
        real, imag = coef[0, here, :].astype(jnp.float32), coef[1, here, :].astype(jnp.float32)
        high, low = split(weight * (real * real + imag * imag))
        kin[i // (2 * ns), (i // ns) % 2, i % ns] = jnp.dot(
            pairs[...], high, preferred_element_type=jnp.float32
        ) + jnp.dot(pairs[...], low, preferred_element_type=jnp.float32)

    loop(0, n, kinetic)
    core_copy = pltpu.make_async_remote_copy(
        kin.at[:, 1 - core], from_core, c_send.at[0], c_recv.at[0],
        device_id=(b + 1 - 2 * core, s), device_id_type=MESH,
    )
    core_copy.start()
    for copy in half_copies:
        copy.wait()
    for fetch in fetches[3:5]:
        fetch.wait()

    def plane(i):
        total = dens[s * zh + i]
        for k in range(ns - 1):
            total = total + half[k, i]
        along = dot3((table_x[0], table_x[1]), split(total.reshape(nx, width)))
        both = split(jnp.concatenate([along[:nx], along[nx:]], axis=1))
        for k in range(ns):
            spec[k, i] = dot3(both, (table_y[0, k], table_y[1, k])).reshape(nb, xl, -1)

    loop(0, zh, plane)

    def spec_copy(k):
        offset = far_first(k, n)
        tb, ts = (b + offset // ns) % nb, (s + offset % ns) % ns
        return pltpu.make_async_remote_copy(
            spec.at[ts, :, tb], scol.at[b, s], s_send.at[k], s_recv.at[k],
            device_id=(tb, ts), device_id_type=MESH,
        )

    loop(0, n - 1, lambda k: spec_copy(k).start())
    scol[b, s] = spec[s, :, b]

    core_copy.wait()

    def add_core(i):
        sum_core[i // ny, i % ny] = kin[i, core] + from_core[i]

    loop(0, nz * ny, add_core)
    plane_copies = []
    for k in range(1, ny * ns):
        ty, ts = (y + k // ns) % ny, (s + k % ns) % ns
        copy = pltpu.make_async_remote_copy(
            sum_core.at[:, ty, ts], from_plane.at[k - 1], p_send.at[k - 1], p_recv.at[k - 1],
            device_id=((z * ny + ty) * 2 + core, ts), device_id_type=MESH,
        )
        copy.start()
        plane_copies.append(copy)

    fetches[5].wait()

    def in_plane(i):
        value = split(dens[i].reshape(nx, width))
        grad_x[i] = dot3((table_g[0, 0], table_g[1, 0]), value)
        grad_y[i] = dot3(value, (table_g[0, 1], table_g[1, 1]))

    loop(0, zl, in_plane)

    fetches[6].wait()
    loop(0, nb - 1, lambda k: column_copy(k).wait())
    for x in range(xl):
        column = split(dcol[:, :, x, :].reshape(nb * zl, width))
        grad[:, :, x, :] = dot3((table_d[0], table_d[1]), column).reshape(nb, zl, width)

    def grad_copy(k):
        to = (b + far_first(k, nb)) % nb
        return pltpu.make_async_remote_copy(
            grad.at[to], gout.at[:, b], g_send.at[k], g_recv.at[k],
            device_id=(to, s), device_id_type=MESH,
        )

    loop(0, nb - 1, lambda k: grad_copy(k).start())
    gout[:, b] = grad[b]

    for copy in plane_copies:
        copy.wait()
    total = sum_core[:, y, s]
    for k in range(1, ny * ns):
        total = total + from_plane[k - 1]
    sum_plane[...] = total

    def line_copy(k):
        tz = (z + k) % nz
        return pltpu.make_async_remote_copy(
            sum_plane.at[tz], from_line.at[k - 1], l_send.at[k - 1], l_recv.at[k - 1],
            device_id=((tz * ny + y) * 2 + core, s), device_id_type=MESH,
        )

    loop(1, nz, lambda k: line_copy(k).start())
    loop(1, nz, lambda k: line_copy(k).wait())
    kweight = sum_plane[z] + jnp.sum(from_line[...], axis=0)
    gk = [spacing * (miller[i].astype(jnp.float32) + kpoint[i]) for i in range(3)]
    kdens[...] = 0.5 * (gk[0] * gk[0] + gk[1] * gk[1] + gk[2] * gk[2]) * kweight
    scaled = kweight * (-1.0 / (n * rows * 128))
    order = ((0, 0), (1, 1), (2, 2), (1, 2), (0, 2), (0, 1))
    part[...] = jnp.zeros_like(part)
    for i, (p, q) in enumerate(order):
        part[pl.ds(i, 1), :] = fold(scaled * gk[p] * gk[q])

    loop(0, n - 1, lambda k: spec_copy(k).wait())
    for fetch in fetches[7:]:
        fetch.wait()
    lanes = scol.shape[4]
    count = lanes // 2
    lane = lax.broadcasted_iota(jnp.int32, (nzg, lanes), 1)
    first = lane < count
    freq_z = axis_frequency(lax.broadcasted_iota(jnp.int32, (nzg, lanes), 0), nzg)
    freq_y = axis_frequency(lane % count + s * count, width)
    row_y = freq_y[:1]
    share = lane * 0 + s
    for x in range(xl):
        column = split(scol[:, :, :, x, :].reshape(nzg, lanes))
        turned = dot3((table_z[0], table_z[1]), column)
        swapped = pltpu.roll(turned[nzg:], count, 1)
        value = turned[:nzg] + jnp.where(first, swapped, -swapped)
        local = jnp.zeros_like(value)
        for k in range(ns):
            left, right = factor[0, :, x, :], factor[1, :, x, :]
            if k > 0:
                left = pltpu.roll(left, width - k * count, 1)
            if k != 1:
                right = pltpu.roll(right, (width - k * count + count) % width, 1)
            local = jnp.where(share == k, jnp.where(first, left, right), local)
        position = jnp.full((nzg, lanes), b * xl + x)
        freq_x = axis_frequency(position, nx)
        length = freq_x * freq_x + freq_y * freq_y + freq_z * freq_z
        positive = length > 0
        inverse = jnp.where(positive, 1.0 / jnp.where(positive, length, 1.0), 0.0)
        hartree = 4.0 * np.pi * value * value * inverse
        weigh = 2.0 * (hartree * inverse + value * local)
        weigh_z = weigh * freq_z
        plain, along_z, along_zz = fold(weigh), fold(weigh_z), fold(weigh_z * freq_z)
        trace = fold(hartree)
        row_x = freq_x[:1]
        terms = (
            plain * row_x * row_x - trace,
            plain * row_y * row_y - trace,
            along_zz - trace,
            along_z * row_y,
            along_z * row_x,
            plain * row_x * row_y,
        )
        for i, term in enumerate(terms):
            part[pl.ds(i, 1), :] += term

    loop(0, nb - 1, lambda k: grad_copy(k).wait())

    def exchange(i):
        value = dens[i].reshape(nx, width)
        g = (grad_x[i], grad_y[i], gout[i].reshape(nx, width))
        total = g[0] * g[0] + g[1] * g[1] + g[2] * g[2]
        square[i] = total
        scale = 4.0 * value * value + 1.0
        weigh = jnp.exp(jnp.log(value) * (-1.0 / 3.0)) * scale / (scale + total)
        weigh = weigh * (-1.0 / (nzg * nx * width))
        for j, (p, q) in enumerate(order):
            part[pl.ds(j, 1), :] += fold(weigh * g[p] * g[q])

    loop(0, zl, exchange)

    def stress_copy(k):
        tb, ts = (b + k // ns) % nb, (s + k % ns) % ns
        return pltpu.make_async_remote_copy(
            part, held.at[k - 1], t_send.at[k - 1], t_recv.at[k - 1],
            device_id=(tb, ts), device_id_type=MESH,
        )

    loop(1, n, lambda k: stress_copy(k).start())
    loop(1, n, lambda k: stress_copy(k).wait())
    stress[...] = part[...] + jnp.sum(held[...], axis=0)


def params(number):
    return pltpu.CompilerParams(
        collective_id=number, has_side_effects=True, vmem_limit_bytes=60 * 2**20
    )


def f32(*shape):
    return jax.ShapeDtypeStruct(shape, jnp.float32)


def shards(nb, ns, coefficients, occupation, miller, density, local_factor):
    dma = pltpu.SemaphoreType.DMA
    _, zl, nx, ny = density.shape
    nzg = zl * nb
    xl = nx // nb
    zh = zl // ns
    part = ny // ns
    lanes = 2 * part
    npw = coefficients.shape[3]
    rows = npw // (nb * ns * 128)
    nbl = coefficients.shape[2]
    fold_y = 2 if nb % 4 == 0 else 1
    fold_z = nb // (2 * fold_y)

    coef = coefficients[0].reshape(2, nbl, npw // 128, 128)
    coef = coef.transpose(0, 2, 1, 3).reshape(2, npw // 128 * nbl, 128)
    pairs = jnp.asarray(np.kron(np.eye(rows), np.ones((1, nbl))), jnp.bfloat16)
    cos_x, sin_x = fourier_tables(nx)
    cos_y, sin_y = fourier_tables(ny)
    cos_z, sin_z = fourier_tables(nzg)
    table_y = []
    for k in range(ns):
        cut = slice(k * part, (k + 1) * part)
        table_y.append(np.block([[cos_y[:, cut], -sin_y[:, cut]], [sin_y[:, cut], cos_y[:, cut]]]))
    in_plane = [derivative_table(nx).astype(np.float64), derivative_table(ny).T.astype(np.float64)]
    fetched = (
        density[0].reshape(zl, nb, xl, ny),
        coef,
        local_factor,
        host_split(np.concatenate([cos_x, -sin_x])),
        host_split(np.stack(table_y)),
        host_split(derivative_table(nzg).astype(np.float64)),
        host_split(np.concatenate([cos_z, sin_z]) / (nzg * nx * ny)),
        host_split(np.stack(in_plane)),
        pairs,
    )

    stress, kinetic_density, square = pl.pallas_call(
        functools.partial(main_kernel, nb, ns, fold_y, fold_z),
        out_shape=(f32(8, 128), f32(rows, 128), f32(zl, nx, ny)),
        in_specs=[pl.BlockSpec(memory_space=pltpu.SMEM), VMEM]
        + [pl.BlockSpec(memory_space=pltpu.HBM)] * len(fetched),
        out_specs=(VMEM,) * 3,
        scratch_shapes=[pltpu.VMEM(value.shape, value.dtype) for value in fetched]
        + [
            pltpu.VMEM(shape, jnp.float32)
            for shape in (
                (fold_z * fold_y, 2, ns, rows, 128),
                (nb, zl, xl, ny),
                (ns - 1, zh, nb, xl, ny),
                (ns, zh, nb, xl, lanes),
                (nb, zl, xl, ny),
                (fold_z * fold_y, ns, rows, 128),
                (fold_z, fold_y, ns, rows, 128),
                (fold_y * ns - 1, fold_z, rows, 128),
                (fold_z, rows, 128),
                (fold_z - 1, rows, 128),
                (nb, ns, zh, xl, lanes),
                (zl, nb, xl, ny),
                (zl, nx, ny),
                (zl, nx, ny),
                (8, 128),
                (nb * ns - 1, 8, 128),
            )
        ]
        + [dma((len(fetched),))]
        + [
            dma((count,))
            for length in (
                nb - 1, ns - 1, 1, fold_y * ns - 1, fold_z - 1, nb * ns - 1, nb - 1, nb * ns - 1,
            )
            for count in (length, length)
        ],
        compiler_params=params(0),
        name="main_exchange",
    )(occupation, miller.reshape(3, rows, 128), *fetched)
    return (
        jnp.sum(stress[:6], axis=1),
        kinetic_density.reshape(rows * 128),
        square[None],
    )


def solution(mesh):
    return jax.shard_map(
        functools.partial(shards, mesh.shape["band"], mesh.shape["spin"]),
        mesh=mesh,
        in_specs=(
            P("spin", None, "band", None),
            P("spin", "band"),
            P(None, ("band", "spin")),
            P("spin", "band", None, None),
            P(None, None, "band", None),
        ),
        out_specs=(P(), P(("band", "spin")), P("spin", "band", None, None)),
        check_vma=False,
    )
```

time: 115 us -> 105 us (0.913)
  other arithmetic: 9.48 us -> 1.3 us
  Pallas kernels: 92.1 us -> 97.4 us
  matrix products: 3.6 us -> 0 us
  local copies, waits for them, and re-layouts: 8.78 us -> 5.41 us
    pallas_call x1, Pallas kernels: 82.8 us -> 97.4 us  [shards(): pl.pallas_call(functools.partial(main_kernel, nb, ns, fold_y, fold_z), ou...]
    pallas_call x1 -> x0, Pallas kernels: 9.23 us -> none  [shards(): pl.pallas_call(functools.partial(third_kernel, nb, ns), out_shape=f32(8,...]
    reduce_sum x5 -> x1, other arithmetic: 5.06 us -> 1.3 us  [shards(): jnp.sum(stress[:6], axis=1)]
    dot_general x3 -> x0, matrix products: 3.6 us -> none  [the longest x1 1.94 us: shards(): jnp.einsum('ik,zxk->zxi', derivative_table(ny), dens, precision=high)]
    squeeze x1 -> x0, other arithmetic: 2.69 us -> none  [shards(): factor = jnp.concatenate([factor[0], factor[1]], axis=2)]
    unnamed x31 -> x3, local copies, waits for them, and re-layouts: 7.58 us -> 5.41 us
where the time goes in v3:
time: 105 us
  Pallas kernels  97.4 us (93%)
  local copies, waits for them, and re-layouts  5.41 us (5%)
  other arithmetic  1.3 us (1%)
    pallas_call x1, Pallas kernels, shards(): pl.pallas_call(functools.partial(main_kernel, nb, ns, fold_y, fold_z), ou...  97.4 us
    unnamed x3, local copies, waits for them, and re-layouts  5.41 us

profile of v3, /device:TPU:0, one launch (start us, length us, event | category | flops | bytes accessed | tf_op | source)
XLA Modules:
  0.0 104.7 jit_solution(13551190522083676025)
XLA Ops:
  0.6 1.6 %copy.17 = s32[1,3,128,128]{3,2,1,0:T(8,128)} copy(s32[1,3,128,128]{3,1,2,0:T(4,128)} %bitcast.16) | data formatting | bytes 393216
  2.3 97.4 %main_exchange.1 = (f32[8,128]{1,0:T(8,128)}, f32[128,128]{1,0:T(8,128)}, f32[16,128,128]{2,1,0:T(8,128)}) custom-call(s32[1,2]{1,0:T(1,128)} %occupation.1, s32[3,128,128]{2,1,0:T(8,128)} %bitcast.15, f32[16,16,8,128]{3,2,1,0:T(8,128)} %bitcast.13, bf16[2,8192,128]{2,1,0:T(8,128)(2,1)} %bitcast.12, f32[2,256,8,128]{3,2,1,0:T(8,128)} %factor_h.1, ...), custom_call_target="tpu_custom_call" | custom-call | tf_op jit(solution)/shard_map/main_exchange/pallas_call | solution.py:376
  99.7 1.3 %slice_reduce_fusion = f32[6]{0:T(128)} fusion(f32[8,128]{1,0:T(8,128)} %get-tuple-element.6), kind=kLoop, calls=%fused_computation.1 | loop fusion | flops 762 | bytes 3096 | tf_op jit(solution)/shard_map/reduce_sum | solution.py:416
  101.0 1.5 %copy.20 = f32[16384]{0:T(1024)} copy(f32[16384]{0:T(1024)} %bitcast.17) | data formatting | bytes 131072
  102.5 2.3 %copy.21 = f32[1,16,128,128]{3,2,1,0:T(8,128)} copy(f32[1,16,128,128]{3,2,1,0:T(8,128)} %bitcast.14) | data formatting | bytes 2097152
